TPU v7x, 256 devices: a whole 4x4x8 slice. The times are simulated.
256 devices in a mesh: gx: 16 (over z, x_lo), gy: 4 (over y), gz: 4 (over x_hi, core).
Axes of the slice: x: 4 (x_hi: 2, x_lo: 2; x = x_hi * 2 + x_lo), y: 4, z: 8, core: 2. Of those that a mesh axis runs over, the one named last changes fastest.
Arguments:
- charges: bfloat16 [64, 16, 16, 32, 128], P('gx', 'gy', 'gz'), may hold values from -6 to 6
- counts: int32 [64, 16, 16], P('gx', 'gy', 'gz'), may hold values from 32 to 128, as said below
- near_offsets: int32 [27, 3], replicated, may hold values from -1 to 1, as said below
- near_blocks: bfloat16 [27, 128, 128], replicated, may hold values from -0.109375 to 0.109375
- leaf_basis: bfloat16 [48, 128], replicated, may hold values from -0.5 to 0.5
- transfer: bfloat16 [8, 48, 48], replicated, may hold values from -0.625 to 0.625
- far_offsets: int32 [2, 32, 3], replicated, may hold values from -2 to 2, as said below
- coupling: bfloat16 [2, 32, 48, 48], replicated, may hold values from -0.15625 to 0.15625
- coarse_coupling: bfloat16 [16, 4, 4, 48, 48], replicated, may hold values from -0.109375 to 0.109375
Outputs:
- potentials: float32 [64, 16, 16, 32, 128], P('gx', 'gy', 'gz')
Inputs may be any that keep to these rules, and one draw needn't show every extreme that they name: `counts`: in each device's block of 4 x 4 x 4 leaf boxes some box holds 128 points. `near_offsets`: each of the 27 offsets with components in -1, 0, 1 appears once. `far_offsets`: each level lists 32 distinct offsets whose largest component in magnitude is 2.
All inputs are finite; a program needn't handle non-finite values.
Results may differ from a plain program's by a relative error of at most 0.008.
Values may be sent and summed in bfloat16 or wider, within the bound.
A program may use at most 128 MiB of HBM per device.

v0:
```python
import jax
import jax.numpy as jnp
from jax import lax
from jax.sharding import PartitionSpec as P


def extended_2(value, sides, width):
    for axis, dim in sides:
        size, length = (lax.axis_size(axis), value.shape[dim])
        up = [(i, (i + 1) % size) for i in range(size)]
        down = [(j, i) for i, j in up]
        last = lax.slice_in_dim(value, length - width, length, axis=dim)
        leading = lax.slice_in_dim(value, 0, width, axis=dim)
        before = lax.ppermute(last, axis, up)
        after = lax.ppermute(leading, axis, down)
        value = jnp.concatenate([before, value, after], axis=dim)
    return value


def take_window(extended, margin, offset, extent):
    start = offset + margin
    corner = [start[0], start[1], start[2]] + [jnp.int32(0)] * (extended.ndim - 3)
    return lax.dynamic_slice(extended, corner, tuple(extent) + tuple(extended.shape[3:]))


def near_field(extended, margin, near_offsets, near_blocks, extent):
    stacked = jax.vmap(lambda offset: take_window(extended, margin, offset, extent))(near_offsets)
    return jnp.einsum("sxyzrq,spq->xyzrp", stacked, near_blocks, preferred_element_type=jnp.float32)


def far_couple(extended, margin, offsets, matrices, extent, rank_count):
    stacked = jax.vmap(lambda offset: take_window(extended, margin, offset, extent))(offsets)
    stacked = stacked.reshape(stacked.shape[:4] + (rank_count, -1))
    return jnp.einsum("kij,kxyzjr->xyzir", matrices, stacked, preferred_element_type=jnp.float32)


def leaf_moments(masked, leaf_basis):
    return jnp.einsum(
        "kp,xyzrp->xyzkr", leaf_basis, masked, preferred_element_type=jnp.float32
    ).astype(jnp.bfloat16)


def flatten(moments):
    return moments.reshape(moments.shape[:3] + (-1,))


def upward(moments, transfer):
    first_len, second_len, third_len, rank_count, columns = moments.shape
    split = moments.reshape(
        first_len // 2, 2, second_len // 2, 2, third_len // 2, 2, rank_count, columns
    )
    kids = split.transpose(0, 2, 4, 1, 3, 5, 6, 7).reshape(
        first_len // 2, second_len // 2, third_len // 2, 8, rank_count, columns
    )
    return jnp.einsum(
        "ckj,xyzcjr->xyzkr", transfer, kids, preferred_element_type=jnp.float32
    ).astype(jnp.bfloat16)


def downward(parent, transfer):
    rounded = parent.astype(jnp.bfloat16)
    kids = jnp.einsum("cjk,xyzjr->xyzckr", transfer, rounded, preferred_element_type=jnp.float32)
    first_len, second_len, third_len, rank_count, columns = parent.shape
    split = kids.reshape(first_len, second_len, third_len, 2, 2, 2, rank_count, columns)
    return split.transpose(0, 3, 1, 4, 2, 5, 6, 7).reshape(
        2 * first_len, 2 * second_len, 2 * third_len, rank_count, columns
    )


def coarse_couple(moments_two, coarse_coupling, place, sizes):
    depth, rank_count, columns = moments_two.shape[2:]
    rows = moments_two.reshape(depth, rank_count * columns)
    index_x, index_y, index_z = place
    count_x, count_y, count_z = sizes
    grid_x, grid_y, grid_z = coarse_coupling.shape[:3]
    flat_coupling = coarse_coupling.reshape(grid_x * grid_y * grid_z, rank_count, rank_count)
    own_z = index_z * depth + jnp.arange(depth, dtype=jnp.int32)
    piece = lax.all_gather(rows, ("gx", "gy", "gz"), axis=0, tiled=True)
    number = jnp.arange(piece.shape[0], dtype=jnp.int32)
    device = number // depth
    source_x = device // (count_y * count_z)
    source_y = device // count_z % count_y
    source_z = device % count_z * depth + number % depth
    off_x = (source_x - index_x) % grid_x
    off_y = (source_y - index_y) % grid_y
    off_z = (source_z[:, None] - own_z[None, :]) % grid_z
    flat_index = (off_x[:, None] * grid_y + off_y[:, None]) * grid_z + off_z
    mats = jnp.take(flat_coupling, flat_index, axis=0)
    values = piece.reshape(piece.shape[0], rank_count, columns)
    local_two = jnp.einsum("acij,ajr->cir", mats, values, preferred_element_type=jnp.float32)
    return local_two.reshape(moments_two.shape)


def body(
    charges,
    counts,
    near_offsets,
    near_blocks,
    leaf_basis,
    transfer,
    far_offsets,
    coupling,
    coarse_coupling,
):
    extent = charges.shape[:3]
    rank_count = leaf_basis.shape[0]
    capacity = charges.shape[4]
    place = (lax.axis_index("gx"), lax.axis_index("gy"), lax.axis_index("gz"))
    sizes = (lax.axis_size("gx"), lax.axis_size("gy"), lax.axis_size("gz"))
    live = (jnp.arange(capacity, dtype=jnp.int32) < counts[..., None]).astype(jnp.bfloat16)
    masked = charges * live[:, :, :, None, :]
    beside = extended_2(masked, (("gx", 0), ("gy", 1), ("gz", 2)), 1)
    own_moments = leaf_moments(masked, leaf_basis)
    moments_wide = extended_2(flatten(own_moments), (("gx", 0), ("gy", 1), ("gz", 2)), 2)
    near = near_field(beside, 1, near_offsets, near_blocks, extent)
    local_zero = far_couple(moments_wide, 2, far_offsets[0], coupling[0], extent, rank_count)
    moments_one = upward(own_moments, transfer)
    wide_one = extended_2(flatten(moments_one), (("gx", 0), ("gy", 1), ("gz", 2)), 2)
    local_one = far_couple(
        wide_one, 2, far_offsets[1], coupling[1], moments_one.shape[:3], rank_count
    )
    moments_two = upward(moments_one, transfer)
    local_two = coarse_couple(moments_two, coarse_coupling, place, sizes)
    total_one = local_one + downward(local_two, transfer)
    total_zero = local_zero + downward(total_one, transfer)
    far = jnp.einsum(
        "kp,xyzkr->xyzrp",
        leaf_basis,
        total_zero.astype(jnp.bfloat16),
        preferred_element_type=jnp.float32,
    )
    return (near + far) * live[:, :, :, None, :].astype(jnp.float32)


def solution(mesh):
    in_specs = (
        P("gx", "gy", "gz", None, None),
        P("gx", "gy", "gz"),
        P(),
        P(),
        P(),
        P(),
        P(),
        P(),
        P(),
    )
    out_specs = P("gx", "gy", "gz", None, None)
    return jax.shard_map(body, mesh=mesh, in_specs=in_specs, out_specs=out_specs, check_vma=False)
```

profile of v0, /device:TPU:2, one launch (start us, length us, event | category | flops | bytes accessed | tf_op | source)
XLA Modules:
  0.0 717.0 jit_solution(14124583641539703596)
XLA Ops:
  27.2 4.5 copy.55
  32.1 339.2 %all-gather = bf16[256,1,1536]{2,1,0:T(2,128)(2,1)S(1)} all-gather(bf16[1,1,1536]{2,1,0:T(2,128)(2,1)S(1)} %reshape.419), channel_id=1, replica_groups=mesh['gx'=16,'gy'=4,'gz'=4] {'gx','gy','gz'}, dimensions={0}, use_global_device_ids=true | all-gather | bytes 789504 | tf_op jit(solution)/shard_map/all_gather | solution.py:78
  371.2 2.8 copy.54
  377.3 15.7 %collective-permute-start.1 = (bf16[1,4,4,32,128]{4,3,2,1,0:T(8,128)(2,1)S(1)}, bf16[1,4,4,32,128]{4,3,2,1,0:T(8,128)(2,1)S(1)}, u32[]{:S(2)}, u32[]{:S(2)}) collective-permute-start(bf16[1,4,4,32,128]{4,3,2,1,0:T(8,128)(2,1)S(1)} %copy-done.15), channel_id=1, source_target_pairs={{16,0},{32,16},{48,32},{64,48},{80,64},{96,80},{112,96},{128,112},... | collective-permute-start | bytes 393224 | tf_op jit(solution)/shard_map/ppermute | solution.py:15
  395.4 3.2 collective-permute-start.15
  400.9 3.1 collective-permute-start.9
  404.4 3.2 collective-permute-start.17
  408.5 3.2 collective-permute-start.3
  413.9 3.2 collective-permute-start.11
  417.9 104.9 %while.3 = (s32[]{:T(128)}, bf16[6,6,6,1536]{3,2,1,0:T(8,128)(2,1)S(1)}, s32[32,4]{0,1:T(4,128)S(1)}, bf16[32,2,2,2,1536]{4,3,2,1,0:T(2,128)(2,1)}, s32[]{:T(128)}) while((s32[]{:T(128)}, bf16[6,6,6,1536]{3,2,1,0:T(8,128)(2,1)S(1)}, s32[32,4]{0,1:T(4,128)S(1)}, bf16[32,2,2,2,1536]{4,3,2,1,0:T(2,128)(2,1)}, s32[]{:T(128)}) %tuple.49), condition=%wide.while_cond.1, body=%wide.while_body.1.sunk | while | flops 2 | bytes 51321 | solution.py:23
  418.6 2.6 bitcast_dynamic-update-slice_fusion.5
  425.1 2.6 bitcast_dynamic-update-slice_fusion.5
  428.4 2.6 bitcast_dynamic-update-slice_fusion.5
  435.0 2.6 bitcast_dynamic-update-slice_fusion.5
  441.5 2.6 bitcast_dynamic-update-slice_fusion.5
  444.8 2.6 bitcast_dynamic-update-slice_fusion.5
  448.1 2.6 bitcast_dynamic-update-slice_fusion.5
  451.3 2.6 bitcast_dynamic-update-slice_fusion.5
  457.9 2.6 bitcast_dynamic-update-slice_fusion.5
  464.5 2.6 bitcast_dynamic-update-slice_fusion.5
  467.7 2.6 bitcast_dynamic-update-slice_fusion.5
  471.0 2.6 bitcast_dynamic-update-slice_fusion.5
  522.8 5.2 reshape.437
  528.9 9.0 %collective-permute-start.4 = (bf16[6,6,1,32,128]{4,3,2,1,0:T(8,128)(2,1)}, bf16[6,6,1,32,128]{4,3,2,1,0:T(8,128)(2,1)}, u32[]{:S(2)}, u32[]{:S(2)}) collective-permute-start(bf16[6,6,1,32,128]{4,3,2,1,0:T(8,128)(2,1)} %get-tuple-element.43), channel_id=1, source_target_pairs={{0,1},{1,2},{2,3},{3,0},{4,5},{5,6},{6,7},{7,4},{8,9},{9,10},{10,1... | collective-permute-start | bytes 884744 | tf_op jit(solution)/shard_map/ppermute | solution.py:14
  537.9 3.2 collective-permute-start.5
  541.1 3.1 fusion.14
  545.4 2.9 collective-permute-done.4
  549.7 7.0 gather_fusion
  556.7 10.2 %fusion.12 = f32[4,4,4,32,128,1]{4,3,2,1,0,5:T(8,128)} fusion(bf16[27,4,4,4,32,128]{5,4,3,2,1,0:T(8,128)(2,1)} %gather_fusion, bf16[27,128,128]{2,1,0:T(8,128)(2,1)} %param.12), kind=kOutput, calls=%fused_computation.29 | convolution fusion | flops 1811939328 | bytes 16089088 | tf_op jit(solution)/shard_map/sxyzrq,spq->xyzrp/dot_general | solution.py:28
  569.4 104.9 %while.2 = (s32[]{:T(128)}, bf16[8,8,8,1536]{3,2,1,0:T(8,128)(2,1)S(1)}, s32[32,4]{0,1:T(4,128)S(1)}, bf16[32,4,4,4,1536]{4,3,2,1,0:T(4,128)(2,1)}, s32[]{:T(128)}) while((s32[]{:T(128)}, bf16[8,8,8,1536]{3,2,1,0:T(8,128)(2,1)S(1)}, s32[32,4]{0,1:T(4,128)S(1)}, bf16[32,4,4,4,1536]{4,3,2,1,0:T(4,128)(2,1)}, s32[]{:T(128)}) %tuple.52), condition=%wide.while_cond, body=%wide.while_body.sunk | while | flops 2 | bytes 395385 | solution.py:23
  570.1 2.6 bitcast_dynamic-update-slice_fusion.4
  573.3 2.6 bitcast_dynamic-update-slice_fusion.4
  576.6 2.6 bitcast_dynamic-update-slice_fusion.4
  579.9 2.6 bitcast_dynamic-update-slice_fusion.4
  583.2 2.6 bitcast_dynamic-update-slice_fusion.4
  586.5 2.6 bitcast_dynamic-update-slice_fusion.4
  589.8 2.6 bitcast_dynamic-update-slice_fusion.4
  593.1 2.6 bitcast_dynamic-update-slice_fusion.4
  596.3 2.6 bitcast_dynamic-update-slice_fusion.4
  599.6 2.6 bitcast_dynamic-update-slice_fusion.4
  602.9 2.6 bitcast_dynamic-update-slice_fusion.4
  606.2 2.6 bitcast_dynamic-update-slice_fusion.4
  609.4 2.6 bitcast_dynamic-update-slice_fusion.4
  612.7 2.6 bitcast_dynamic-update-slice_fusion.4
  616.0 2.6 bitcast_dynamic-update-slice_fusion.4
  619.3 2.6 bitcast_dynamic-update-slice_fusion.4
  622.5 2.6 bitcast_dynamic-update-slice_fusion.4
  625.8 2.6 bitcast_dynamic-update-slice_fusion.4
  629.1 2.6 bitcast_dynamic-update-slice_fusion.4
  632.4 2.6 bitcast_dynamic-update-slice_fusion.4
  635.7 2.6 bitcast_dynamic-update-slice_fusion.4
  639.0 2.6 bitcast_dynamic-update-slice_fusion.4
  642.2 2.6 bitcast_dynamic-update-slice_fusion.4
  645.5 2.6 bitcast_dynamic-update-slice_fusion.4
  648.8 2.6 bitcast_dynamic-update-slice_fusion.4
  652.1 2.6 bitcast_dynamic-update-slice_fusion.4
  655.3 2.6 bitcast_dynamic-update-slice_fusion.4
  658.6 2.6 bitcast_dynamic-update-slice_fusion.4
  661.9 2.6 bitcast_dynamic-update-slice_fusion.4
  665.2 2.6 bitcast_dynamic-update-slice_fusion.4
  668.4 2.6 bitcast_dynamic-update-slice_fusion.4
  671.7 2.6 bitcast_dynamic-update-slice_fusion.4
  674.3 28.9 %reshape.436 = bf16[32,4,4,4,48,32]{5,4,3,2,1,0:T(8,128)(2,1)} reshape(bf16[32,4,4,4,1536]{4,3,2,1,0:T(4,128)(2,1)} %get-tuple-element.12) | data formatting | bytes 12582912 | tf_op jit(solution)/shard_map/reshape | solution.py:33
  703.3 12.1 %fusion.2 = bf16[4,4,4,48,32]{3,4,2,1,0:T(8,128)(2,1)S(1)} fusion(f32[4,4,4,48,32]{3,4,2,1,0:T(8,128)} %bitcast.188, bf16[32,4,4,4,48,32]{5,4,3,2,1,0:T(8,128)(2,1)} %reshape.436, bf16[2,32,48,48]{3,2,1,0:T(8,128)(2,1)} %param.16), kind=kOutput, calls=%fused_computation.12 | convolution fusion | flops 302186496 | bytes 26804224 | tf_op jit(solution)/shard_map/kij,kxyzjr->xyzir/dot_general | solution.py:34
  (269 shorter events, 141.2 us)
Async XLA Ops:
  0.0 22.2 %copy-start = (bf16[16,4,4,48,48]{4,3,2,1,0:T(8,128)(2,1)S(1)}, bf16[16,4,4,48,48]{4,3,2,1,0:T(8,128)(2,1)}, u32[]{:S(2)}) copy-start(bf16[16,4,4,48,48]{4,3,2,1,0:T(8,128)(2,1)} %param.17) | copy-start | bytes 3538948
  0.0 5.4 copy-start.6
  2.8 0.8 copy-start.2
  4.5 0.8 copy-start.4
  4.5 17.6 %copy-start.18 = (s32[2,32,3]{1,0,2:T(2,128)S(1)}, s32[2,32,3]{1,0,2:T(2,128)}, u32[]{:S(2)}) copy-start(s32[2,32,3]{1,0,2:T(2,128)} %param.15) | copy-start | bytes 2308
  5.7 5.0 copy-start.13
  6.5 370.7 %collective-permute-start.12 = (bf16[2,2,2,1536]{3,2,1,0:T(2,128)(2,1)}, bf16[2,2,2,1536]{3,2,1,0:T(2,128)(2,1)}, u32[]{:S(2)}, u32[]{:S(2)}) collective-permute-start(bf16[2,2,2,1536]{3,2,1,0:T(2,128)(2,1)} %reshape.343), channel_id=1, source_target_pairs={{0,16},{16,32},{32,48},{48,64},{64,80},{80,96},{96,112},{112,128},... | collective-permute-start | bytes 73736 | tf_op jit(solution)/shard_map/ppermute | solution.py:14
  8.4 386.1 %collective-permute-start.13 = (bf16[2,2,2,1536]{3,2,1,0:T(2,128)(2,1)}, bf16[2,2,2,1536]{3,2,1,0:T(2,128)(2,1)}, u32[]{:S(2)}, u32[]{:S(2)}) collective-permute-start(bf16[2,2,2,1536]{3,2,1,0:T(2,128)(2,1)} %reshape.343), channel_id=1, source_target_pairs={{16,0},{32,16},{48,32},{64,48},{80,64},{96,80},{112,96},{128,112},... | collective-permute-start | bytes 73736 | tf_op jit(solution)/shard_map/ppermute | solution.py:15
  12.7 382.6 %collective-permute-start.6 = (bf16[2,4,4,1536]{3,2,1,0:T(4,128)(2,1)}, bf16[2,4,4,1536]{3,2,1,0:T(4,128)(2,1)}, u32[]{:S(2)}, u32[]{:S(2)}) collective-permute-start(bf16[2,4,4,1536]{3,2,1,0:T(4,128)(2,1)} %slice.91), channel_id=1, source_target_pairs={{0,16},{16,32},{32,48},{48,64},{64,80},{80,96},{96,112},{112,128},... | collective-permute-start | bytes 294920 | tf_op jit(solution)/shard_map/ppermute | solution.py:14
  17.4 382.2 %collective-permute-start.7 = (bf16[2,4,4,1536]{3,2,1,0:T(4,128)(2,1)}, bf16[2,4,4,1536]{3,2,1,0:T(4,128)(2,1)}, u32[]{:S(2)}, u32[]{:S(2)}) collective-permute-start(bf16[2,4,4,1536]{3,2,1,0:T(4,128)(2,1)} %slice.93), channel_id=1, source_target_pairs={{16,0},{32,16},{48,32},{64,48},{80,64},{96,80},{112,96},{128,112},... | collective-permute-start | bytes 294920 | tf_op jit(solution)/shard_map/ppermute | solution.py:15
  21.6 382.8 %collective-permute-start = (bf16[1,4,4,32,128]{4,3,2,1,0:T(8,128)(2,1)}, bf16[1,4,4,32,128]{4,3,2,1,0:T(8,128)(2,1)S(1)}, u32[]{:S(2)}, u32[]{:S(2)}) collective-permute-start(bf16[1,4,4,32,128]{4,3,2,1,0:T(8,128)(2,1)} %get-tuple-element.51), channel_id=1, source_target_pairs={{0,16},{16,32},{32,48},{48,64},{64,80},{80,96},{96,112},{112,128},... | collective-permute-start | bytes 393224 | tf_op jit(solution)/shard_map/ppermute | solution.py:14
  27.2 4.6 copy-start.7
  27.2 4.6 copy-start.14
  31.7 342.4 %copy-start.19 = (s32[27,3]{0,1:T(4,128)S(1)}, s32[27,3]{0,1:T(4,128)}, u32[]{:S(2)}) copy-start(s32[27,3]{0,1:T(4,128)} %param.11) | copy-start | bytes 976
  31.7 344.5 %copy-start.5 = (bf16[4,4,4,32,48]{4,3,2,1,0:T(8,128)(2,1)S(1)}, bf16[4,4,4,32,48]{4,3,2,1,0:T(8,128)(2,1)}, u32[]{:S(2)}) copy-start(bf16[4,4,4,32,48]{4,3,2,1,0:T(8,128)(2,1)} %copy-done.4) | copy-start | bytes 589828
  371.2 6.0 copy-start.15
  374.1 33.6 %copy-start.3 = (bf16[4,4,4,32,128]{4,3,2,1,0:T(8,128)(2,1)S(1)}, bf16[4,4,4,32,128]{4,3,2,1,0:T(8,128)(2,1)}, u32[]{:S(2)}) copy-start(bf16[4,4,4,32,128]{4,3,2,1,0:T(8,128)(2,1)} %copy-done.2) | copy-start | bytes 1572868
  377.3 30.4 %collective-permute-start.1 = (bf16[1,4,4,32,128]{4,3,2,1,0:T(8,128)(2,1)S(1)}, bf16[1,4,4,32,128]{4,3,2,1,0:T(8,128)(2,1)S(1)}, u32[]{:S(2)}, u32[]{:S(2)}) collective-permute-start(bf16[1,4,4,32,128]{4,3,2,1,0:T(8,128)(2,1)S(1)} %copy-done.15), channel_id=1, source_target_pairs={{16,0},{32,16},{48,32},{64,48},{80,64},{96,80},{112,96},{128,112},... | collective-permute-start | bytes 393224 | tf_op jit(solution)/shard_map/ppermute | solution.py:15
  395.3 5.6 collective-permute-start.14
  395.4 8.7 %collective-permute-start.15 = (bf16[6,2,2,1536]{3,2,1,0:T(2,128)(2,1)S(1)}, bf16[6,2,2,1536]{3,2,1,0:T(2,128)(2,1)S(1)}, u32[]{:S(2)}, u32[]{:S(2)}) collective-permute-start(bf16[6,2,2,1536]{3,2,1,0:T(2,128)(2,1)S(1)} %constant_dynamic-update-slice_fusion.3), channel_id=1, source_target_pairs={{4,0},{8,4},{12,8},{0,12},{5,1},{9,5},{13,9},{1,13},{6,2},{10,6},{... | collective-permute-start | bytes 221192 | tf_op jit(solution)/shard_map/ppermute | solution.py:15
  400.7 7.8 %collective-permute-start.8 = (bf16[8,2,4,1536]{3,2,1,0:T(4,128)(2,1)S(1)}, bf16[8,2,4,1536]{3,2,1,0:T(4,128)(2,1)S(1)}, u32[]{:S(2)}, u32[]{:S(2)}) collective-permute-start(bf16[8,2,4,1536]{3,2,1,0:T(4,128)(2,1)S(1)} %get-tuple-element.53), channel_id=1, source_target_pairs={{0,4},{4,8},{8,12},{12,0},{1,5},{5,9},{9,13},{13,1},{2,6},{6,10},{... | collective-permute-start | bytes 589832 | tf_op jit(solution)/shard_map/ppermute | solution.py:14
  400.9 10.8 %collective-permute-start.9 = (bf16[8,2,4,1536]{3,2,1,0:T(4,128)(2,1)S(1)}, bf16[8,2,4,1536]{3,2,1,0:T(4,128)(2,1)S(1)}, u32[]{:S(2)}, u32[]{:S(2)}) collective-permute-start(bf16[8,2,4,1536]{3,2,1,0:T(4,128)(2,1)S(1)} %get-tuple-element.54), channel_id=1, source_target_pairs={{4,0},{8,4},{12,8},{0,12},{5,1},{9,5},{13,9},{1,13},{6,2},{10,6},{... | collective-permute-start | bytes 589832 | tf_op jit(solution)/shard_map/ppermute | solution.py:15
  404.3 9.6 %collective-permute-start.16 = (bf16[6,6,2,1536]{3,2,1,0:T(2,128)(2,1)S(1)}, bf16[6,6,2,1536]{3,2,1,0:T(2,128)(2,1)S(1)}, u32[]{:S(2)}, u32[]{:S(2)}) collective-permute-start(bf16[6,6,2,1536]{3,2,1,0:T(2,128)(2,1)S(1)} %pad_maximum_fusion.9), channel_id=1, source_target_pairs={{0,1},{1,2},{2,3},{3,0},{4,5},{5,6},{6,7},{7,4},{8,9},{9,10},{10,1... | collective-permute-start | bytes 663560 | tf_op jit(solution)/shard_map/ppermute | solution.py:14
  404.4 12.7 %collective-permute-start.17 = (bf16[6,6,2,1536]{3,2,1,0:T(2,128)(2,1)S(1)}, bf16[6,6,2,1536]{3,2,1,0:T(2,128)(2,1)S(1)}, u32[]{:S(2)}, u32[]{:S(2)}) collective-permute-start(bf16[6,6,2,1536]{3,2,1,0:T(2,128)(2,1)S(1)} %pad_maximum_fusion.9), channel_id=1, source_target_pairs={{1,0},{2,1},{3,2},{0,3},{5,4},{6,5},{7,6},{4,7},{9,8},{10,9},{11,1... | collective-permute-start | bytes 663560 | tf_op jit(solution)/shard_map/ppermute | solution.py:15
  408.5 119.5 %collective-permute-start.2 = (bf16[6,1,4,32,128]{4,3,2,1,0:T(8,128)(2,1)}, bf16[6,1,4,32,128]{4,3,2,1,0:T(8,128)(2,1)S(1)}, u32[]{:S(2)}, u32[]{:S(2)}) collective-permute-start(bf16[6,1,4,32,128]{4,3,2,1,0:T(8,128)(2,1)} %get-tuple-element.47), channel_id=1, source_target_pairs={{0,4},{4,8},{8,12},{12,0},{1,5},{5,9},{9,13},{13,1},{2,6},{6,10},{... | collective-permute-start | bytes 589832 | tf_op jit(solution)/shard_map/ppermute | solution.py:14
  408.5 119.5 %collective-permute-start.3 = (bf16[6,1,4,32,128]{4,3,2,1,0:T(8,128)(2,1)}, bf16[6,1,4,32,128]{4,3,2,1,0:T(8,128)(2,1)S(1)}, u32[]{:S(2)}, u32[]{:S(2)}) collective-permute-start(bf16[6,1,4,32,128]{4,3,2,1,0:T(8,128)(2,1)} %get-tuple-element.48), channel_id=1, source_target_pairs={{4,0},{8,4},{12,8},{0,12},{5,1},{9,5},{13,9},{1,13},{6,2},{10,6},{... | collective-permute-start | bytes 589832 | tf_op jit(solution)/shard_map/ppermute | solution.py:15
  411.7 5.4 copy-start.9
  413.9 153.1 %collective-permute-start.10 = (bf16[8,8,2,1536]{3,2,1,0:T(2,128)(2,1)}, bf16[8,8,2,1536]{3,2,1,0:T(2,128)(2,1)}, u32[]{:S(2)}, u32[]{:S(2)}) collective-permute-start(bf16[8,8,2,1536]{3,2,1,0:T(2,128)(2,1)} %get-tuple-element.45), channel_id=1, source_target_pairs={{0,1},{1,2},{2,3},{3,0},{4,5},{5,6},{6,7},{7,4},{8,9},{9,10},{10,1... | collective-permute-start | bytes 1179656 | tf_op jit(solution)/shard_map/ppermute | solution.py:14
  413.9 153.1 %collective-permute-start.11 = (bf16[8,8,2,1536]{3,2,1,0:T(2,128)(2,1)}, bf16[8,8,2,1536]{3,2,1,0:T(2,128)(2,1)}, u32[]{:S(2)}, u32[]{:S(2)}) collective-permute-start(bf16[8,8,2,1536]{3,2,1,0:T(2,128)(2,1)} %get-tuple-element.46), channel_id=1, source_target_pairs={{1,0},{2,1},{3,2},{0,3},{5,4},{6,5},{7,6},{4,7},{9,8},{10,9},{11,1... | collective-permute-start | bytes 1179656 | tf_op jit(solution)/shard_map/ppermute | solution.py:15
  528.0 13.2 %copy-start.11 = (bf16[6,1,4,32,128]{4,3,2,1,0:T(8,128)(2,1)}, bf16[6,1,4,32,128]{4,3,2,1,0:T(8,128)(2,1)S(1)}, u32[]{:S(2)}) copy-start(bf16[6,1,4,32,128]{4,3,2,1,0:T(8,128)(2,1)S(1)} %collective-permute-done.2) | copy-start | bytes 589828
  528.0 16.3 %copy-start.12 = (bf16[6,1,4,32,128]{4,3,2,1,0:T(8,128)(2,1)}, bf16[6,1,4,32,128]{4,3,2,1,0:T(8,128)(2,1)S(1)}, u32[]{:S(2)}) copy-start(bf16[6,1,4,32,128]{4,3,2,1,0:T(8,128)(2,1)S(1)} %collective-permute-done.3) | copy-start | bytes 589828
  528.9 19.3 %collective-permute-start.4 = (bf16[6,6,1,32,128]{4,3,2,1,0:T(8,128)(2,1)}, bf16[6,6,1,32,128]{4,3,2,1,0:T(8,128)(2,1)}, u32[]{:S(2)}, u32[]{:S(2)}) collective-permute-start(bf16[6,6,1,32,128]{4,3,2,1,0:T(8,128)(2,1)} %get-tuple-element.43), channel_id=1, source_target_pairs={{0,1},{1,2},{2,3},{3,0},{4,5},{5,6},{6,7},{7,4},{8,9},{9,10},{10,1... | collective-permute-start | bytes 884744 | tf_op jit(solution)/shard_map/ppermute | solution.py:14
  537.9 10.3 %collective-permute-start.5 = (bf16[6,6,1,32,128]{4,3,2,1,0:T(8,128)(2,1)}, bf16[6,6,1,32,128]{4,3,2,1,0:T(8,128)(2,1)}, u32[]{:S(2)}, u32[]{:S(2)}) collective-permute-start(bf16[6,6,1,32,128]{4,3,2,1,0:T(8,128)(2,1)} %get-tuple-element.44), channel_id=1, source_target_pairs={{1,0},{2,1},{3,2},{0,3},{5,4},{6,5},{7,6},{4,7},{9,8},{10,9},{11,1... | collective-permute-start | bytes 884744 | tf_op jit(solution)/shard_map/ppermute | solution.py:15
  556.7 10.3 %copy-start.10 = (bf16[8,2,4,1536]{3,2,1,0:T(4,128)(2,1)S(1)}, bf16[8,2,4,1536]{3,2,1,0:T(4,128)(2,1)}, u32[]{:S(2)}) copy-start(bf16[8,2,4,1536]{3,2,1,0:T(4,128)(2,1)} %copy-done.9) | copy-start | bytes 589828
  703.3 12.2 %copy-start.8 = (f32[4,4,4,32,128,1]{4,3,2,1,0,5:T(8,128)S(1)}, f32[4,4,4,32,128,1]{4,3,2,1,0,5:T(8,128)}, u32[]{:S(2)}) copy-start(f32[4,4,4,32,128,1]{4,3,2,1,0,5:T(8,128)} %fusion.12) | copy-start | bytes 3145732
  703.3 12.2 %copy-start.16 = (f32[4,4,4,128]{3,1,0,2:T(4,128)S(1)}, f32[4,4,4,128]{3,1,0,2:T(4,128)}, u32[]{:S(2)}) copy-start(f32[4,4,4,128]{3,1,0,2:T(4,128)} %get-tuple-element.55) | copy-start | bytes 98308
  703.3 12.2 %copy-start.17 = (bf16[48,128]{1,0:T(8,128)(2,1)S(1)}, bf16[48,128]{1,0:T(8,128)(2,1)}, u32[]{:S(2)}) copy-start(bf16[48,128]{1,0:T(8,128)(2,1)} %param.13) | copy-start | bytes 36868
  703.3 13.5 %copy-start.1 = (bf16[16,4,4,48,48]{4,3,2,1,0:T(8,128)(2,1)S(1)}, bf16[16,4,4,48,48]{4,3,2,1,0:T(8,128)(2,1)}, u32[]{:S(2)}) copy-start(bf16[16,4,4,48,48]{4,3,2,1,0:T(8,128)(2,1)} %param.17) | copy-start | bytes 3538948
where the time goes:
time: 725 us; the launch traced here: 717 us
  blocking collectives  339 us (47%)
  local copies, waits for them, and re-layouts  281 us (39%)
  starting transfers between devices  52 us (7%)
  matrix products  29.3 us (4%)
  other arithmetic  11.4 us (2%)
    all_gather x1, blocking collectives, coarse_couple(): piece = lax.all_gather(rows, ('gx', 'gy', 'gz'), axis=0, tiled=True)  339 us
    gather x192, local copies, waits for them, and re-layouts  210 us
    ppermute x9, starting transfers between devices, extended_2(): after = lax.ppermute(leading, axis, down)  37.8 us
    reshape x2, local copies, waits for them, and re-layouts, far_couple(): stacked = stacked.reshape(stacked.shape[:4] + (rank_count, -1))  34.1 us
  transfers between devices with their start and end apart: 18, of which 2 were waited for; matrix products, arithmetic and copies ran while one was open for 23% of the time, Pallas kernels for 0%

commit v1 on v0

v1 whole, which is shorter than its diff:
```python
import functools

import jax
import jax.numpy as jnp
from jax import lax
from jax.experimental import pallas as pl
from jax.experimental.pallas import tpu as pltpu
from jax.sharding import PartitionSpec as P

MESH = pl.DeviceIdType.MESH
PLANE = [(dx, dz) for dx in (-1, 0, 1) for dz in (-1, 0, 1) if (dx, dz) != (0, 0)]
BF = jnp.bfloat16
F32 = jnp.float32

FIELD_E = ((1, 5, 1), (1, 5, 1), (1, 5, 1))
FIELD_M = ((2, 6, 2), (1, 3, 1), (1, 3, 1))
FIELD_L = ((2, 4, 2), (1, 2, 1), (1, 2, 1))


def source_range(axis, step):
    low, high, width = axis
    if step == 0:
        return pl.ds(low, high - low)
    return pl.ds(high - width, width) if step > 0 else pl.ds(low, width)


def target_range(axis, step):
    low, high, width = axis
    if step == 0:
        return pl.ds(low, high - low)
    return pl.ds(low - width, width) if step > 0 else pl.ds(high, width)


def dot(a, b, contract_a=1, contract_b=0):
    return lax.dot_general(
        a, b, (((contract_a,), (contract_b,)), ((), ())), preferred_element_type=F32
    )


def pack(value):
    zero = jnp.zeros((16, 32), value.dtype)
    return jnp.concatenate([value[0:16], value[16:32], value[32:48], zero], axis=1)


def unpack(value):
    return jnp.concatenate([value[:, 0:32], value[:, 32:64], value[:, 64:96]], axis=0)


def kernel(
    sizes,
    counts,
    near_off,
    far_off,
    charges,
    near_blocks,
    basis_hbm,
    transfer_hbm,
    coupling_hbm,
    coarse_hbm,
    out,
    ext,
    mom,
    one,
    raw,
    blocks,
    basis,
    transfer,
    coupling,
    coarse,
    toep,
    packed,
    near,
    gathered,
    part_out,
    part_in,
    down,
    inverse,
    base,
    in_sem,
    send_sem,
    recv_sem,
    g_send,
    g_recv,
    p_send,
    p_recv,
):
    nx, ny, nz = sizes
    mx, my, mz = lax.axis_index("gx"), lax.axis_index("gy"), lax.axis_index("gz")

    def device(dx, dy, dz):
        return {
            "gx": lax.rem(mx + (dx + nx), nx),
            "gy": lax.rem(my + (dy + ny), ny),
            "gz": lax.rem(mz + (dz + nz), nz),
        }

    loads = [
        pltpu.make_async_copy(src, dst, in_sem.at[i])
        for i, (src, dst) in enumerate(
            (
                (charges, raw),
                (basis_hbm, basis),
                (transfer_hbm, transfer),
                (near_blocks, blocks),
                (coarse_hbm, coarse),
                (coupling_hbm, coupling),
            )
        )
    ]
    for copy in loads:
        copy.start()

    barrier = pltpu.get_barrier_semaphore()
    for dx, dz in PLANE:
        if dx != 0 and dz != 0:
            pl.semaphore_signal(barrier, inc=1, device_id=device(dx, 0, dz), device_id_type=MESH)

    def greet_line(d, carry):
        pl.semaphore_signal(barrier, inc=1, device_id=device(d, 0, 0), device_id_type=MESH)
        return carry

    lax.fori_loop(1, nx, greet_line, 0)

    def greet_plane(d, carry):
        pl.semaphore_signal(
            barrier, inc=1, device_id=device(0, d // nz, d % nz), device_id_type=MESH
        )
        return carry

    lax.fori_loop(1, ny * nz, greet_plane, 0)

    bufs = (ext, mom.at[0], one.at[0])
    fields = (FIELD_E, FIELD_M, FIELD_L)

    def remote(src, dst, sem, target):
        return pltpu.make_async_remote_copy(
            src_ref=src,
            dst_ref=dst,
            send_sem=send_sem.at[sem],
            recv_sem=recv_sem.at[sem],
            device_id=target,
            device_id_type=MESH,
        )

    def plane_copy(f, number):
        dx, dz = PLANE[number]
        ax, ay, az = fields[f]
        mid = source_range(ay, 0)
        return remote(
            bufs[f].at[source_range(ax, dx), mid, source_range(az, dz)],
            bufs[f].at[target_range(ax, dx), mid, target_range(az, dz)],
            18 * f + number,
            device(dx, 0, dz),
        )

    def slab_copy(f, dy, piece):
        ax, ay, az = fields[f]
        full_z = pl.ds(0, az[1] + az[2])
        regions = (
            (source_range(ax, 0), source_range(az, 0)),
            (target_range(ax, 1), full_z),
            (target_range(ax, -1), full_z),
            (source_range(ax, 0), target_range(az, 1)),
            (source_range(ax, 0), target_range(az, -1)),
        )
        rx, rz = regions[piece]
        return remote(
            bufs[f].at[rx, source_range(ay, dy), rz],
            bufs[f].at[rx, target_range(ay, dy), rz],
            18 * f + 8 + 5 * (dy > 0) + piece,
            device(0, dy, 0),
        )

    plane = [[plane_copy(f, n) for n in range(8)] for f in range(3)]
    slab = [[[slab_copy(f, dy, p) for p in range(5)] for dy in (-1, 1)] for f in range(3)]

    def start_own(f):
        for dy in range(2):
            slab[f][dy][0].start()
        for copy in plane[f]:
            copy.start()

    def forward(f):
        groups = (
            (1, [n for n, (dx, dz) in enumerate(PLANE) if dx == 1]),
            (2, [n for n, (dx, dz) in enumerate(PLANE) if dx == -1]),
            (3, [PLANE.index((0, 1))]),
            (4, [PLANE.index((0, -1))]),
        )
        for piece, needed in groups:
            for n in needed:
                plane[f][n].wait_recv()
            for dy in range(2):
                slab[f][dy][piece].start()

    def finish(f):
        for dy in range(2):
            for piece in range(5):
                slab[f][dy][piece].wait_recv()

    loads[0].wait()
    lane = lax.broadcasted_iota(jnp.int32, (32, 128), 1)

    def mask_x(x, carry):
        for y in range(4):
            for z in range(4):
                live = (lane < counts[x, y, z]).astype(F32).astype(BF)
                ext[x + 1, y + 1, z + 1] = raw[x, y, z] * live
        return carry

    lax.fori_loop(0, 4, mask_x, 0)
    pl.semaphore_wait(barrier, (nx - 1) + (ny * nz - 1) + 4)
    start_own(0)

    loads[1].wait()
    loads[2].wait()

    def leaf_x(x, carry):
        for yp in range(2):
            for zp in range(2):
                box = ext[x + 1, pl.ds(2 * yp + 1, 2), pl.ds(2 * zp + 1, 2)]
                value = dot(basis[...], box.reshape(128, 128), 1, 1)
                mom[0, x + 2, yp + 1, zp + 1] = value.astype(BF)
        return carry

    lax.fori_loop(0, 4, leaf_x, 0)
    start_own(1)

    for cx in range(2):
        acc = jnp.zeros((48, 128), F32)
        for i in range(2):
            quads = [mom[0, 2 * cx + i + 2, cy + 1, cz + 1] for cy in range(2) for cz in range(2)]
            for jl in range(4):
                kids = jnp.concatenate([q[:, 32 * jl : 32 * jl + 32] for q in quads], axis=1)
                acc = acc + dot(transfer[4 * i + jl], kids)
        one[0, cx + 2, 1, 1] = acc.astype(BF)
    start_own(2)

    acc = jnp.zeros((48, 32), F32)
    for i in range(2):
        own = one[0, i + 2, 1, 1]
        for jl in range(4):
            acc = acc + dot(transfer[4 * i + jl], own[:, 32 * jl : 32 * jl + 32])
    gathered[0] = pack(acc).astype(BF)

    def gather_copy(d):
        return pltpu.make_async_remote_copy(
            src_ref=gathered.at[0],
            dst_ref=gathered.at[d],
            send_sem=g_send.at[d],
            recv_sem=g_recv.at[d],
            device_id=device(d, 0, 0),
            device_id_type=MESH,
        )

    def gather_start(d, carry):
        gather_copy(d).start()
        return carry

    lax.fori_loop(1, nx, gather_start, 0)

    codes = [9 * near_off[0, s] + 3 * near_off[1, s] + near_off[2, s] + 13 for s in range(27)]
    for s in range(27):
        inverse[27 + s] = codes[s]

    def invert(c, carry):
        found = jnp.int32(0)
        for s in range(27):
            found = jnp.where(inverse[27 + s] == c, jnp.int32(s), found)
        inverse[c] = found
        return carry

    lax.fori_loop(0, 27, invert, 0)
    for level in range(2):
        for e in range(32):
            ox = far_off[0, level, e] + 2
            ay = far_off[1, level, e] + 2
            az = far_off[2, level, e] + 2
            half_y, half_z = lax.shift_right_logical(ay, 1), lax.shift_right_logical(az, 1)
            kind = 2 * (ay - 2 * half_y) + (az - 2 * half_z)
            if level == 0:
                base[e] = ((kind * 8 + ox) * 4 + half_y) * 4 + half_z
            else:
                base[32 + e] = ((kind * 6 + ox) * 3 + half_y) * 3 + half_z

    loads[3].wait()

    def build(c, carry):
        taps = [blocks[inverse[3 * c + t]].T for t in range(3)]
        zero = jnp.zeros((128, 128), BF)
        toep[c, 0:128, 0:128] = taps[0]
        toep[c, 0:128, 128:256] = zero
        toep[c, 128:256, 0:128] = taps[1]
        toep[c, 128:256, 128:256] = taps[0]
        toep[c, 256:384, 0:128] = taps[2]
        toep[c, 256:384, 128:256] = taps[1]
        toep[c, 384:512, 0:128] = zero
        toep[c, 384:512, 128:256] = taps[2]
        return carry

    lax.fori_loop(0, 9, build, 0)

    loads[5].wait()
    for level in range(2):
        for e in range(32):
            packed[level, :, 48 * e : 48 * e + 48] = coupling[level, e]

    loads[4].wait()

    def gather_wait(d, carry):
        gather_copy(d).wait_recv()
        return carry

    lax.fori_loop(1, nx, gather_wait, 0)

    def partial(dy, carry):
        acc = jnp.zeros((192, 32), F32)
        for d in range(nx):
            mats = coarse[(nx - d) % nx, dy].reshape(192, 48)
            acc = acc + dot(mats, unpack(gathered[d]))
        for dz in range(4):
            part_out[4 * dy + dz] = pack(acc[48 * dz : 48 * dz + 48])
        return carry

    lax.fori_loop(0, 4, partial, 0)

    def part_copy(d):
        return pltpu.make_async_remote_copy(
            src_ref=part_out.at[d],
            dst_ref=part_in.at[d],
            send_sem=p_send.at[d],
            recv_sem=p_recv.at[d],
            device_id=device(0, -(d // nz), -(d % nz)),
            device_id_type=MESH,
        )

    def part_start(d, carry):
        part_copy(d).start()
        return carry

    lax.fori_loop(1, ny * nz, part_start, 0)

    for f in range(3):
        forward(f)

    def lhs(x, ys, count):
        parts = []
        for step in range(3):
            rows = [
                jnp.concatenate([ext[x + step, pl.ds(ys, count), 2 * zp + j] for j in range(4)], axis=2)
                for zp in range(2)
            ]
            stacked = jnp.stack(rows, axis=1)
            parts.append(stacked.reshape(count * 64, 512))
        return parts

    def near_x(x, carry):
        for dy, ys, count, row in ((1, 1, 4, 0), (0, 1, 3, 1), (2, 2, 3, 0)):
            acc = sum(dot(v, toep[3 * step + dy]) for step, v in enumerate(lhs(x, ys, count)))
            acc = acc.reshape(count, 64, 256)
            if dy == 1:
                near[x] = acc
            else:
                near[x, row : row + 3] += acc
        return carry

    lax.fori_loop(0, 4, near_x, 0)

    finish(2)

    def shifts(buf, xs, side, x):
        def ahead_z(a, b):
            return jnp.concatenate([a[:, 32:64], b[:, 0:32], a[:, 96:128], b[:, 64:96]], axis=1)

        def ahead_y(a, b):
            return jnp.concatenate([a[:, 64:128], b[:, 0:64]], axis=1)

        for yp in range(side):
            for zp in range(side - 1):
                buf[1, x, yp, zp] = ahead_z(buf[0, x, yp, zp], buf[0, x, yp, zp + 1])
        for yp in range(side - 1):
            for zp in range(side):
                buf[2, x, yp, zp] = ahead_y(buf[0, x, yp, zp], buf[0, x, yp + 1, zp])
        for yp in range(side - 1):
            for zp in range(side - 1):
                buf[3, x, yp, zp] = ahead_y(buf[1, x, yp, zp], buf[1, x, yp + 1, zp])

    def shift_one(x, carry):
        shifts(one, 6, 3, x)
        return carry

    lax.fori_loop(0, 6, shift_one, 0)
    flat_one = one.reshape(4 * 6 * 3 * 3, 48, 128)
    sides = []
    for cx in range(2):
        sides.append(
            jnp.concatenate([flat_one[base[32 + e] + cx * 9] for e in range(32)], axis=0)
        )
    local_one = dot(packed[1], jnp.concatenate(sides, axis=1))

    def part_wait(d, carry):
        part_copy(d).wait_recv()
        return carry

    lax.fori_loop(1, ny * nz, part_wait, 0)
    total = part_out[0]
    for d in range(1, ny * nz):
        total = total + part_in[d]
    local_two = unpack(total).astype(BF)
    for cx in range(2):
        spread = jnp.concatenate(
            [dot(transfer[4 * cx + jl], local_two, 0, 0) for jl in range(4)], axis=1
        )
        total_one = (local_one[:, 128 * cx : 128 * cx + 128] + spread).astype(BF)
        for i in range(2):
            pieces = [dot(transfer[4 * i + jl], total_one, 0, 0) for jl in range(4)]
            for quad in range(4):
                down[2 * cx + i, quad] = jnp.concatenate(
                    [p[:, 32 * quad : 32 * quad + 32] for p in pieces], axis=1
                )

    finish(0)
    for dy, ext_y, y in ((0, 0, 0), (2, 5, 3)):
        acc = jnp.zeros((256, 256), F32)
        for step in range(3):
            rows = [
                jnp.concatenate([ext[pl.ds(step, 4), ext_y, 2 * zp + j] for j in range(4)], axis=2)
                for zp in range(2)
            ]
            acc = acc + dot(jnp.stack(rows, axis=1).reshape(256, 512), toep[3 * step + dy])
        near[:, y] += acc.reshape(4, 64, 256)

    finish(1)

    def shift_mom(x, carry):
        shifts(mom, 8, 4, x)
        return carry

    lax.fori_loop(0, 8, shift_mom, 0)
    flat_mom = mom.reshape(4 * 8 * 4 * 4, 48, 128)

    def leaf_level(t, carry):
        x, yp = t // 2, t % 2
        offset = x * 16 + yp * 4
        sides = [
            jnp.concatenate([flat_mom[base[e] + (offset + zp)] for e in range(32)], axis=0)
            for zp in range(2)
        ]
        local = dot(packed[0], jnp.concatenate(sides, axis=1))
        for zp in range(2):
            total = (local[:, 128 * zp : 128 * zp + 128] + down[x, 2 * yp + zp]).astype(BF)
            far = dot(total, basis[...], 0, 0)
            for y2 in range(2):
                for z2 in range(2):
                    y, z = 2 * yp + y2, 2 * zp + z2
                    live = lane < counts[x, y, z]
                    row = 64 * y2 + 32 * z2
                    value = near[x, y, 32 * zp : 32 * zp + 32, 128 * z2 : 128 * z2 + 128]
                    out[x, y, z] = jnp.where(live, value + far[row : row + 32], 0.0)
        return carry

    lax.fori_loop(0, 8, leaf_level, 0)

    for f in range(3):
        for copy in plane[f]:
            copy.wait_send()
        for dy in range(2):
            for copy in slab[f][dy]:
                copy.wait_send()

    def sent_line(d, carry):
        gather_copy(d).wait_send()
        return carry

    lax.fori_loop(1, nx, sent_line, 0)

    def sent_plane(d, carry):
        part_copy(d).wait_send()
        return carry

    lax.fori_loop(1, ny * nz, sent_plane, 0)


def body(
    sizes,
    charges,
    counts,
    near_offsets,
    near_blocks,
    leaf_basis,
    transfer,
    far_offsets,
    coupling,
    coarse_coupling,
):
    smem = pl.BlockSpec(memory_space=pltpu.SMEM)
    hbm = pl.BlockSpec(memory_space=pl.ANY)
    vmem = pl.BlockSpec(memory_space=pltpu.VMEM)
    dma = pltpu.SemaphoreType.DMA
    nx, ny, nz = sizes
    return pl.pallas_call(
        functools.partial(kernel, sizes),
        out_shape=jax.ShapeDtypeStruct((4, 4, 4, 32, 128), F32),
        in_specs=[smem] * 3 + [hbm] * 6,
        out_specs=vmem,
        scratch_shapes=[
            pltpu.VMEM((6, 6, 6, 32, 128), BF),
            pltpu.VMEM((4, 8, 4, 4, 48, 128), BF),
            pltpu.VMEM((4, 6, 3, 3, 48, 128), BF),
            pltpu.VMEM((4, 4, 4, 32, 128), BF),
            pltpu.VMEM((27, 128, 128), BF),
            pltpu.VMEM((48, 128), BF),
            pltpu.VMEM((8, 48, 48), BF),
            pltpu.VMEM((2, 32, 48, 48), BF),
            pltpu.VMEM((16, 4, 4, 48, 48), BF),
            pltpu.VMEM((9, 512, 256), BF),
            pltpu.VMEM((2, 48, 1536), BF),
            pltpu.VMEM((4, 4, 64, 256), F32),
            pltpu.VMEM((nx, 16, 128), BF),
            pltpu.VMEM((ny * nz, 16, 128), F32),
            pltpu.VMEM((ny * nz, 16, 128), F32),
            pltpu.VMEM((4, 4, 48, 128), F32),
            pltpu.SMEM((64,), jnp.int32),
            pltpu.SMEM((64,), jnp.int32),
            dma((6,)),
            dma((54,)),
            dma((54,)),
            dma((nx,)),
            dma((nx,)),
            dma((ny * nz,)),
            dma((ny * nz,)),
        ],
        compiler_params=pltpu.CompilerParams(
            collective_id=0, has_side_effects=True, vmem_limit_bytes=60 * 1024 * 1024
        ),
    )(
        counts,
        near_offsets.T,
        far_offsets.transpose(2, 0, 1),
        charges,
        near_blocks,
        leaf_basis,
        transfer,
        coupling,
        coarse_coupling,
    )


def solution(mesh):
    sizes = (mesh.shape["gx"], mesh.shape["gy"], mesh.shape["gz"])
    spread = P("gx", "gy", "gz", None, None)
    in_specs = (spread, P("gx", "gy", "gz"), P(), P(), P(), P(), P(), P(), P())
    return jax.shard_map(
        functools.partial(body, sizes),
        mesh=mesh,
        in_specs=in_specs,
        out_specs=spread,
        check_vma=False,
    )
```

time: 725 us -> 67.9 us (0.09); the launches traced: 717 us -> 67.8 us
  blocking collectives: 339 us -> 0 us
  local copies, waits for them, and re-layouts: 281 us -> 2.29 us
  Pallas kernels: 0 us -> 65.5 us
  starting transfers between devices: 52 us -> 0 us
  matrix products: 29.3 us -> 0 us
  other arithmetic: 11.4 us -> 0 us
    all_gather x1 -> x0, blocking collectives: 339 us -> none  [coarse_couple(): piece = lax.all_gather(rows, ('gx', 'gy', 'gz'), axis=0, tiled=True)]
    gather x194 -> x0, local copies, waits for them, and re-layouts: 219 us -> none
    pallas_call x0 -> x1, Pallas kernels: none -> 65.5 us  [body(): pl.pallas_call(functools.partial(kernel, sizes), out_shape=jax.ShapeDtype...]
    ppermute x18 -> x0, starting transfers between devices: 52 us -> none  [the longest x9 37.8 us: extended_2(): after = lax.ppermute(leading, axis, down)]
    reshape x5 -> x0, local copies, waits for them, and re-layouts: 36.5 us -> none  [the longest x2 34.1 us: far_couple(): stacked = stacked.reshape(stacked.shape[:4] + (rank_count, -1))]
    dot_general x8 -> x0, matrix products: 29.3 us -> none  [the longest x1 12.1 us: far_couple(): jnp.einsum('kij,kxyzjr->xyzir', matrices, stacked, preferred_element_type...]
    slice x8 -> x0, local copies, waits for them, and re-layouts: 9.52 us -> none  [the longest x5 5.53 us: extended_2(): last = lax.slice_in_dim(value, length - width, length, axis=dim)]
  transfers between devices with their start and end apart: 18 -> 0, of which waited for: 2 -> 0; matrix products, arithmetic and copies ran while one was open for 23% -> 0% of each run, Pallas kernels for 0% -> 0%
where the time goes in v1:
time: 67.9 us; the launch traced here: 67.8 us
  Pallas kernels  65.5 us (96%)
  local copies, waits for them, and re-layouts  2.29 us (3%)
    pallas_call x1, Pallas kernels, body(): pl.pallas_call(functools.partial(kernel, sizes), out_shape=jax.ShapeDtype...  65.5 us
    unnamed x1, local copies, waits for them, and re-layouts  2.29 us

profile of v1, /device:TPU:2, one launch (start us, length us, event | category | flops | bytes accessed | tf_op | source)
XLA Modules:
  0.0 67.8 jit_solution(18445379432035729226)
XLA Ops:
  0.0 65.5 %shard_map.91 = f32[4,4,4,32,128]{4,3,2,1,0:T(8,128)} custom-call(s32[4,4,4]{2,1,0:T(4,128)} %counts.1, s32[3,27]{1,0:T(4,128)} %bitcast.3, s32[3,2,32]{2,1,0:T(2,128)} %bitcast.2, bf16[4,4,4,32,128]{4,3,2,1,0:T(8,128)(2,1)} %charges.1, bf16[27,128,128]{2,1,0:T(8,128)(2,1)} %near_blocks.1, bf16[48,128]{1,0:T(8,128)(2,1)} %basis_hbm.1, ...), custom_call_target="tpu_custom_call" | custom-call | tf_op jit(solution)/shard_map/pallas_call | solution.py:501
  65.5 2.3 %copy.11 = f32[4,4,4,32,128]{4,3,2,1,0:T(8,128)} copy(f32[4,4,4,32,128]{4,3,2,1,0:T(8,128)} %shard_map.91) | data formatting | bytes 2097152

commit v2 on v1

--- a/solution.py
+++ b/solution.py
@@ -8,26 +8,28 @@
 from jax.sharding import PartitionSpec as P
 
 MESH = pl.DeviceIdType.MESH
-PLANE = [(dx, dz) for dx in (-1, 0, 1) for dz in (-1, 0, 1) if (dx, dz) != (0, 0)]
 BF = jnp.bfloat16
 F32 = jnp.float32
 
-FIELD_E = ((1, 5, 1), (1, 5, 1), (1, 5, 1))
-FIELD_M = ((2, 6, 2), (1, 3, 1), (1, 3, 1))
-FIELD_L = ((2, 4, 2), (1, 2, 1), (1, 2, 1))
-
-
-def source_range(axis, step):
+FIELDS = (
+    ((1, 5, 1), (1, 5, 1), (1, 5, 1)),
+    ((2, 6, 2), (1, 3, 1), (1, 3, 1)),
+    ((2, 4, 2), (1, 2, 1), (1, 2, 1)),
+)
+SEMS = 18
+
+
+def own(axis):
+    return pl.ds(axis[0], axis[1] - axis[0])
+
+
+def source(axis, step):
     low, high, width = axis
-    if step == 0:
-        return pl.ds(low, high - low)
     return pl.ds(high - width, width) if step > 0 else pl.ds(low, width)
 
 
-def target_range(axis, step):
+def target(axis, step):
     low, high, width = axis
-    if step == 0:
-        return pl.ds(low, high - low)
     return pl.ds(low - width, width) if step > 0 else pl.ds(high, width)
 
 
@@ -70,6 +72,7 @@
     toep,
     packed,
     near,
+    result,
     gathered,
     part_out,
     part_in,
@@ -77,6 +80,7 @@
     inverse,
     base,
     in_sem,
+    out_sem,
     send_sem,
     recv_sem,
     g_send,
@@ -86,6 +90,9 @@
 ):
     nx, ny, nz = sizes
     mx, my, mz = lax.axis_index("gx"), lax.axis_index("gy"), lax.axis_index("gz")
+
+    odd = lax.rem(mz, 2)
+    flip = 2 * odd - 1
 
     def device(dx, dy, dz):
         return {
@@ -111,9 +118,8 @@
         copy.start()
 
     barrier = pltpu.get_barrier_semaphore()
-    for dx, dz in PLANE:
-        if dx != 0 and dz != 0:
-            pl.semaphore_signal(barrier, inc=1, device_id=device(dx, 0, dz), device_id_type=MESH)
+    for dx in (-1, 1):
+        pl.semaphore_signal(barrier, inc=1, device_id=device(dx, 0, flip), device_id_type=MESH)
 
     def greet_line(d, carry):
         pl.semaphore_signal(barrier, inc=1, device_id=device(d, 0, 0), device_id_type=MESH)
@@ -130,73 +136,101 @@
     lax.fori_loop(1, ny * nz, greet_plane, 0)
 
     bufs = (ext, mom.at[0], one.at[0])
-    fields = (FIELD_E, FIELD_M, FIELD_L)
-
-    def remote(src, dst, sem, target):
+
+    def remote(f, sem, to, src, dst):
         return pltpu.make_async_remote_copy(
-            src_ref=src,
-            dst_ref=dst,
-            send_sem=send_sem.at[sem],
-            recv_sem=recv_sem.at[sem],
-            device_id=target,
+            src_ref=bufs[f].at[src],
+            dst_ref=bufs[f].at[dst],
+            send_sem=send_sem.at[SEMS * f + sem],
+            recv_sem=recv_sem.at[SEMS * f + sem],
+            device_id=to,
             device_id_type=MESH,
         )
 
-    def plane_copy(f, number):
-        dx, dz = PLANE[number]
-        ax, ay, az = fields[f]
-        mid = source_range(ay, 0)
-        return remote(
-            bufs[f].at[source_range(ax, dx), mid, source_range(az, dz)],
-            bufs[f].at[target_range(ax, dx), mid, target_range(az, dz)],
-            18 * f + number,
-            device(dx, 0, dz),
-        )
-
-    def slab_copy(f, dy, piece):
-        ax, ay, az = fields[f]
-        full_z = pl.ds(0, az[1] + az[2])
-        regions = (
-            (source_range(ax, 0), source_range(az, 0)),
-            (target_range(ax, 1), full_z),
-            (target_range(ax, -1), full_z),
-            (source_range(ax, 0), target_range(az, 1)),
-            (source_range(ax, 0), target_range(az, -1)),
-        )
-        rx, rz = regions[piece]
-        return remote(
-            bufs[f].at[rx, source_range(ay, dy), rz],
-            bufs[f].at[rx, target_range(ay, dy), rz],
-            18 * f + 8 + 5 * (dy > 0) + piece,
-            device(0, dy, 0),
-        )
-
-    plane = [[plane_copy(f, n) for n in range(8)] for f in range(3)]
-    slab = [[[slab_copy(f, dy, p) for p in range(5)] for dy in (-1, 1)] for f in range(3)]
-
-    def start_own(f):
-        for dy in range(2):
-            slab[f][dy][0].start()
-        for copy in plane[f]:
+    def copies(f):
+        ax, ay, az = FIELDS[f]
+        low, high, width = az
+        span = high - low
+        wide = span + width
+        outer_src = pl.ds(low + odd * (span - width), width)
+        inner_src = pl.ds(high - width - odd * (span - width), width)
+        outer_dst = pl.ds(low - width + odd * wide, width)
+        inner_dst = pl.ds(high - odd * wide, width)
+        own_outer = pl.ds(low - width + odd * width, wide)
+        plane = {}
+        for dx in (-1, 0, 1):
+            rx = (source(ax, dx), target(ax, dx)) if dx else (own(ax), own(ax))
+            if dx:
+                plane[dx, 0] = remote(
+                    f, (dx + 1) // 2, device(dx, 0, 0),
+                    (rx[0], own(ay), own(az)), (rx[1], own(ay), own(az)),
+                )
+            plane[dx, 1] = remote(
+                f, 3 + dx, device(dx, 0, flip),
+                (rx[0], own(ay), outer_src), (rx[1], own(ay), inner_dst),
+            )
+        slab = {}
+        regions = {
+            "own": (own(ax), own(az)),
+            "low": (target(ax, 1), own_outer),
+            "high": (target(ax, -1), own_outer),
+            "outer": (own(ax), outer_dst),
+        }
+        for j, dy in enumerate((-1, 1)):
+            for i, (name, (rx, rz)) in enumerate(regions.items()):
+                slab[dy, name] = remote(
+                    f, 5 + 4 * j + i, device(0, dy, 0),
+                    (rx, source(ay, dy), rz), (rx, target(ay, dy), rz),
+                )
+        side = {}
+        full = pl.ds(0, ax[1] + ax[2])
+        regions = {
+            "own": (own(ax), own(ay)),
+            "low": (target(ax, 1), own(ay)),
+            "high": (target(ax, -1), own(ay)),
+            1: (full, target(ay, 1)),
+            -1: (full, target(ay, -1)),
+        }
+        for i, (name, (rx, ry)) in enumerate(regions.items()):
+            side[name] = remote(
+                f, 13 + i, device(0, 0, -flip), (rx, ry, inner_src), (rx, ry, outer_dst)
+            )
+        return plane, slab, side
+
+    planes, slabs, sides = zip(*[copies(f) for f in range(3)])
+
+    def start_slab(f):
+        for dy in (-1, 1):
+            slabs[f][dy, "own"].start()
+
+    def start_plane(f):
+        sides[f]["own"].start()
+        for copy in planes[f].values():
             copy.start()
 
     def forward(f):
-        groups = (
-            (1, [n for n, (dx, dz) in enumerate(PLANE) if dx == 1]),
-            (2, [n for n, (dx, dz) in enumerate(PLANE) if dx == -1]),
-            (3, [PLANE.index((0, 1))]),
-            (4, [PLANE.index((0, -1))]),
-        )
-        for piece, needed in groups:
-            for n in needed:
-                plane[f][n].wait_recv()
-            for dy in range(2):
-                slab[f][dy][piece].start()
+        for name, dx in (("low", 1), ("high", -1)):
+            planes[f][dx, 0].wait_recv()
+            sides[f][name].start()
+            planes[f][dx, 1].wait_recv()
+            for dy in (-1, 1):
+                slabs[f][dy, name].start()
+        planes[f][0, 1].wait_recv()
+        for dy in (-1, 1):
+            slabs[f][dy, "outer"].start()
+
+    def hand_over(f):
+        for dy in (-1, 1):
+            for name in ("own", "low", "high"):
+                slabs[f][dy, name].wait_recv()
+            sides[f][dy].start()
 
     def finish(f):
-        for dy in range(2):
-            for piece in range(5):
-                slab[f][dy][piece].wait_recv()
+        for dy in (-1, 1):
+            slabs[f][dy, "outer"].wait_recv()
+        for name, copy in sides[f].items():
+            if f != 0 or name in (-1, 1):
+                copy.wait_recv()
 
     loads[0].wait()
     lane = lax.broadcasted_iota(jnp.int32, (32, 128), 1)
@@ -209,8 +243,6 @@
         return carry
 
     lax.fori_loop(0, 4, mask_x, 0)
-    pl.semaphore_wait(barrier, (nx - 1) + (ny * nz - 1) + 4)
-    start_own(0)
 
     loads[1].wait()
     loads[2].wait()
@@ -224,7 +256,6 @@
         return carry
 
     lax.fori_loop(0, 4, leaf_x, 0)
-    start_own(1)
 
     for cx in range(2):
         acc = jnp.zeros((48, 128), F32)
@@ -234,13 +265,12 @@
                 kids = jnp.concatenate([q[:, 32 * jl : 32 * jl + 32] for q in quads], axis=1)
                 acc = acc + dot(transfer[4 * i + jl], kids)
         one[0, cx + 2, 1, 1] = acc.astype(BF)
-    start_own(2)
 
     acc = jnp.zeros((48, 32), F32)
     for i in range(2):
-        own = one[0, i + 2, 1, 1]
+        box = one[0, i + 2, 1, 1]
         for jl in range(4):
-            acc = acc + dot(transfer[4 * i + jl], own[:, 32 * jl : 32 * jl + 32])
+            acc = acc + dot(transfer[4 * i + jl], box[:, 32 * jl : 32 * jl + 32])
     gathered[0] = pack(acc).astype(BF)
 
     def gather_copy(d):
@@ -257,7 +287,14 @@
         gather_copy(d).start()
         return carry
 
+    pl.semaphore_wait(barrier, (nx - 1) + (ny * nz - 1) + 2)
     lax.fori_loop(1, nx, gather_start, 0)
+    start_plane(1)
+    start_slab(1)
+    start_plane(2)
+    start_slab(2)
+    start_plane(0)
+    start_slab(0)
 
     codes = [9 * near_off[0, s] + 3 * near_off[1, s] + near_off[2, s] + 13 for s in range(27)]
     for s in range(27):
@@ -340,63 +377,73 @@
 
     lax.fori_loop(1, ny * nz, part_start, 0)
 
-    for f in range(3):
-        forward(f)
-
-    def lhs(x, ys, count):
-        parts = []
-        for step in range(3):
-            rows = [
-                jnp.concatenate([ext[x + step, pl.ds(ys, count), 2 * zp + j] for j in range(4)], axis=2)
-                for zp in range(2)
-            ]
-            stacked = jnp.stack(rows, axis=1)
-            parts.append(stacked.reshape(count * 64, 512))
-        return parts
-
-    def near_x(x, carry):
-        for dy, ys, count, row in ((1, 1, 4, 0), (0, 1, 3, 1), (2, 2, 3, 0)):
-            acc = sum(dot(v, toep[3 * step + dy]) for step, v in enumerate(lhs(x, ys, count)))
-            acc = acc.reshape(count, 64, 256)
-            if dy == 1:
-                near[x] = acc
-            else:
-                near[x, row : row + 3] += acc
-        return carry
-
-    lax.fori_loop(0, 4, near_x, 0)
+    forward(1)
+    forward(2)
+
+    group = lax.broadcasted_iota(jnp.int32, (48, 128), 1)
+    even_z = (group % 64) < 32
+    first_y = group < 64
+
+    def shifts(buf, side, x):
+        def ahead_y(a, b):
+            return jnp.where(first_y, pltpu.roll(a, 64, 1), pltpu.roll(b, 64, 1))
+
+        plain = [[buf[0, x, yp, zp] for zp in range(side)] for yp in range(side)]
+        moved = []
+        for yp in range(side):
+            down_z = [pltpu.roll(v, 96, 1) for v in plain[yp][:-1]]
+            up_z = [pltpu.roll(v, 32, 1) for v in plain[yp][1:]]
+            moved.append([jnp.where(even_z, a, b) for a, b in zip(down_z, up_z)])
+            for zp in range(side - 1):
+                buf[1, x, yp, zp] = moved[yp][zp]
+        for kind, rows in ((2, plain), (3, moved)):
+            turned = [[pltpu.roll(v, 64, 1) for v in row] for row in rows]
+            for yp in range(side - 1):
+                for zp in range(len(rows[0])):
+                    buf[kind, x, yp, zp] = jnp.where(
+                        first_y, turned[yp][zp], turned[yp + 1][zp]
+                    )
+
+    hand_over(1)
+    finish(1)
+
+    def shift_mom(x, carry):
+        shifts(mom, 4, x)
+        return carry
+
+    lax.fori_loop(0, 8, shift_mom, 0)
+    flat_mom = mom.reshape(4 * 8 * 4 * 4, 48, 128)
+
+    def leaf_list(t, carry):
+        x, yp = t // 2, t % 2
+        offset = x * 16 + yp * 4
+        windows = [
+            jnp.concatenate([flat_mom[base[e] + (offset + zp)] for e in range(32)], axis=0)
+            for zp in range(2)
+        ]
+        local = dot(packed[0], jnp.concatenate(windows, axis=1))
+        for zp in range(2):
+            down[x, 2 * yp + zp] = local[:, 128 * zp : 128 * zp + 128]
+        return carry
+
+    lax.fori_loop(0, 4, leaf_list, 0)
+    hand_over(2)
+    forward(0)
+    lax.fori_loop(4, 8, leaf_list, 0)
 
     finish(2)
 
-    def shifts(buf, xs, side, x):
-        def ahead_z(a, b):
-            return jnp.concatenate([a[:, 32:64], b[:, 0:32], a[:, 96:128], b[:, 64:96]], axis=1)
-
-        def ahead_y(a, b):
-            return jnp.concatenate([a[:, 64:128], b[:, 0:64]], axis=1)
-
-        for yp in range(side):
-            for zp in range(side - 1):
-                buf[1, x, yp, zp] = ahead_z(buf[0, x, yp, zp], buf[0, x, yp, zp + 1])
-        for yp in range(side - 1):
-            for zp in range(side):
-                buf[2, x, yp, zp] = ahead_y(buf[0, x, yp, zp], buf[0, x, yp + 1, zp])
-        for yp in range(side - 1):
-            for zp in range(side - 1):
-                buf[3, x, yp, zp] = ahead_y(buf[1, x, yp, zp], buf[1, x, yp + 1, zp])
-
     def shift_one(x, carry):
-        shifts(one, 6, 3, x)
+        shifts(one, 3, x)
         return carry
 
     lax.fori_loop(0, 6, shift_one, 0)
     flat_one = one.reshape(4 * 6 * 3 * 3, 48, 128)
-    sides = []
-    for cx in range(2):
-        sides.append(
-            jnp.concatenate([flat_one[base[32 + e] + cx * 9] for e in range(32)], axis=0)
-        )
-    local_one = dot(packed[1], jnp.concatenate(sides, axis=1))
+    windows = [
+        jnp.concatenate([flat_one[base[32 + e] + cx * 9] for e in range(32)], axis=0)
+        for cx in range(2)
+    ]
+    local_one = dot(packed[1], jnp.concatenate(windows, axis=1))
 
     def part_wait(d, carry):
         part_copy(d).wait_recv()
@@ -415,9 +462,58 @@
         for i in range(2):
             pieces = [dot(transfer[4 * i + jl], total_one, 0, 0) for jl in range(4)]
             for quad in range(4):
-                down[2 * cx + i, quad] = jnp.concatenate(
+                down[2 * cx + i, quad] += jnp.concatenate(
                     [p[:, 32 * quad : 32 * quad + 32] for p in pieces], axis=1
                 )
+
+    def far_x(x, carry):
+        for yp in range(2):
+            for zp in range(2):
+                far = dot(down[x, 2 * yp + zp].astype(BF), basis[...], 0, 0)
+                for y2 in range(2):
+                    for z2 in range(2):
+                        row = 64 * y2 + 32 * z2
+                        near[
+                            x, 2 * yp + y2, 32 * zp : 32 * zp + 32, 128 * z2 : 128 * z2 + 128
+                        ] = far[row : row + 32]
+        return carry
+
+    lax.fori_loop(0, 4, far_x, 0)
+
+    for name in ("own", "low", "high"):
+        sides[0][name].wait_recv()
+
+    def lhs(x, ys, count):
+        parts = []
+        for step in range(3):
+            rows = [
+                jnp.concatenate([ext[x + step, pl.ds(ys, count), 2 * zp + j] for j in range(4)], axis=2)
+                for zp in range(2)
+            ]
+            stacked = jnp.stack(rows, axis=1)
+            parts.append(stacked.reshape(count * 64, 512))
+        return parts
+
+    def near_x(x, carry):
+        for dy, ys, count, row in ((1, 1, 4, 0), (0, 1, 3, 1), (2, 2, 3, 0)):
+            acc = sum(dot(v, toep[3 * step + dy]) for step, v in enumerate(lhs(x, ys, count)))
+            near[x, row : row + count] += acc.reshape(count, 64, 256)
+        return carry
+
+    lax.fori_loop(0, 4, near_x, 0)
+    hand_over(0)
+
+    def write(y):
+        for x in range(4):
+            for z in range(4):
+                zp, z2 = z // 2, z % 2
+                value = near[x, y, 32 * zp : 32 * zp + 32, 128 * z2 : 128 * z2 + 128]
+                result[x, y, z] = jnp.where(lane < counts[x, y, z], value, 0.0)
+        copy = pltpu.make_async_copy(result.at[:, y], out.at[:, y], out_sem.at[y])
+        copy.start()
+        return copy
+
+    stores = [write(1), write(2)]
 
     finish(0)
     for dy, ext_y, y in ((0, 0, 0), (2, 5, 3)):
@@ -429,43 +525,13 @@
             ]
             acc = acc + dot(jnp.stack(rows, axis=1).reshape(256, 512), toep[3 * step + dy])
         near[:, y] += acc.reshape(4, 64, 256)
-
-    finish(1)
-
-    def shift_mom(x, carry):
-        shifts(mom, 8, 4, x)
-        return carry
-
-    lax.fori_loop(0, 8, shift_mom, 0)
-    flat_mom = mom.reshape(4 * 8 * 4 * 4, 48, 128)
-
-    def leaf_level(t, carry):
-        x, yp = t // 2, t % 2
-        offset = x * 16 + yp * 4
-        sides = [
-            jnp.concatenate([flat_mom[base[e] + (offset + zp)] for e in range(32)], axis=0)
-            for zp in range(2)
-        ]
-        local = dot(packed[0], jnp.concatenate(sides, axis=1))
-        for zp in range(2):
-            total = (local[:, 128 * zp : 128 * zp + 128] + down[x, 2 * yp + zp]).astype(BF)
-            far = dot(total, basis[...], 0, 0)
-            for y2 in range(2):
-                for z2 in range(2):
-                    y, z = 2 * yp + y2, 2 * zp + z2
-                    live = lane < counts[x, y, z]
-                    row = 64 * y2 + 32 * z2
-                    value = near[x, y, 32 * zp : 32 * zp + 32, 128 * z2 : 128 * z2 + 128]
-                    out[x, y, z] = jnp.where(live, value + far[row : row + 32], 0.0)
-        return carry
-
-    lax.fori_loop(0, 8, leaf_level, 0)
+        stores.append(write(y))
+    for copy in stores:
+        copy.wait()
 
     for f in range(3):
-        for copy in plane[f]:
-            copy.wait_send()
-        for dy in range(2):
-            for copy in slab[f][dy]:
+        for group in (planes[f], slabs[f], sides[f]):
+            for copy in group.values():
                 copy.wait_send()
 
     def sent_line(d, carry):
@@ -495,14 +561,13 @@
 ):
     smem = pl.BlockSpec(memory_space=pltpu.SMEM)
     hbm = pl.BlockSpec(memory_space=pl.ANY)
-    vmem = pl.BlockSpec(memory_space=pltpu.VMEM)
     dma = pltpu.SemaphoreType.DMA
     nx, ny, nz = sizes
     return pl.pallas_call(
         functools.partial(kernel, sizes),
         out_shape=jax.ShapeDtypeStruct((4, 4, 4, 32, 128), F32),
         in_specs=[smem] * 3 + [hbm] * 6,
-        out_specs=vmem,
+        out_specs=hbm,
         scratch_shapes=[
             pltpu.VMEM((6, 6, 6, 32, 128), BF),
             pltpu.VMEM((4, 8, 4, 4, 48, 128), BF),
@@ -516,6 +581,7 @@
             pltpu.VMEM((9, 512, 256), BF),
             pltpu.VMEM((2, 48, 1536), BF),
             pltpu.VMEM((4, 4, 64, 256), F32),
+            pltpu.VMEM((4, 4, 4, 32, 128), F32),
             pltpu.VMEM((nx, 16, 128), BF),
             pltpu.VMEM((ny * nz, 16, 128), F32),
             pltpu.VMEM((ny * nz, 16, 128), F32),
@@ -523,8 +589,9 @@
             pltpu.SMEM((64,), jnp.int32),
             pltpu.SMEM((64,), jnp.int32),
             dma((6,)),
-            dma((54,)),
-            dma((54,)),
+            dma((4,)),
+            dma((3 * SEMS,)),
+            dma((3 * SEMS,)),
             dma((nx,)),
             dma((nx,)),
             dma((ny * nz,)),

time: 67.9 us -> 47.2 us (0.70)
  Pallas kernels: 65.5 us -> 44.3 us
    pallas_call x1, Pallas kernels: 65.5 us -> 44.3 us  [body(): pl.pallas_call(functools.partial(kernel, sizes), out_shape=jax.ShapeDtype...]
where the time goes in v2:
time: 47.2 us; the launch traced here: 46.6 us
  Pallas kernels  44.3 us (94%)
  local copies, waits for them, and re-layouts  2.29 us (5%)
    pallas_call x1, Pallas kernels, body(): pl.pallas_call(functools.partial(kernel, sizes), out_shape=jax.ShapeDtype...  44.3 us
    unnamed x1, local copies, waits for them, and re-layouts  2.29 us

profile of v2, /device:TPU:2, one launch (start us, length us, event | category | flops | bytes accessed | tf_op | source)
XLA Modules:
  0.0 46.6 jit_solution(9224766858593411921)
XLA Ops:
  0.0 44.3 %shard_map.91 = f32[4,4,4,32,128]{4,3,2,1,0:T(8,128)} custom-call(s32[4,4,4]{2,1,0:T(4,128)} %counts.1, s32[3,27]{1,0:T(4,128)} %bitcast.3, s32[3,2,32]{2,1,0:T(2,128)} %bitcast.2, bf16[4,4,4,32,128]{4,3,2,1,0:T(8,128)(2,1)} %charges.1, bf16[27,128,128]{2,1,0:T(8,128)(2,1)} %near_blocks.1, bf16[48,128]{1,0:T(8,128)(2,1)} %basis_hbm.1, ...), custom_call_target="tpu_custom_call" | custom-call | tf_op jit(solution)/shard_map/pallas_call | solution.py:566
  44.3 2.3 %copy.11 = f32[4,4,4,32,128]{4,3,2,1,0:T(8,128)} copy(f32[4,4,4,32,128]{4,3,2,1,0:T(8,128)} %shard_map.91) | data formatting | bytes 2097152

commit v3 on v2

--- a/solution.py
+++ b/solution.py
@@ -205,8 +205,8 @@
 
     def start_plane(f):
         sides[f]["own"].start()
-        for copy in planes[f].values():
-            copy.start()
+        for step in ((-1, 0), (1, 0), (-1, 1), (1, 1), (0, 1)):
+            planes[f][step].start()
 
     def forward(f):
         for name, dx in (("low", 1), ("high", -1)):
@@ -215,9 +215,15 @@
             planes[f][dx, 1].wait_recv()
             for dy in (-1, 1):
                 slabs[f][dy, name].start()
+
+    def forward_outer(f):
         planes[f][0, 1].wait_recv()
         for dy in (-1, 1):
             slabs[f][dy, "outer"].start()
+
+    def middle(f):
+        for name in ("own", "low", "high"):
+            sides[f][name].wait_recv()
 
     def hand_over(f):
         for dy in (-1, 1):
@@ -228,9 +234,7 @@
     def finish(f):
         for dy in (-1, 1):
             slabs[f][dy, "outer"].wait_recv()
-        for name, copy in sides[f].items():
-            if f != 0 or name in (-1, 1):
-                copy.wait_recv()
+            sides[f][dy].wait_recv()
 
     loads[0].wait()
     lane = lax.broadcasted_iota(jnp.int32, (32, 128), 1)
@@ -337,6 +341,24 @@
 
     lax.fori_loop(0, 9, build, 0)
 
+    def boxes(xs, ys, zs):
+        parts = [ext[xs, ys, z] for z in zs]
+        rows = parts[0].shape[0] * parts[0].shape[1] * 32
+        return jnp.concatenate(parts, axis=3).reshape(rows, 128 * len(zs))
+
+    INNER = {1: (0, 4, 1), 0: (1, 3, 1), 2: (0, 3, 2)}
+    for dx, (xo, count_x, xi) in INNER.items():
+        for dy, (yo, count_y, yi) in INNER.items():
+            for zp, zs, rows in ((0, (1, 2, 3), pl.ds(128, 384)), (1, (2, 3, 4), pl.ds(0, 384))):
+                value = dot(
+                    boxes(pl.ds(xi, count_x), pl.ds(yi, count_y), zs), toep[3 * dx + dy, rows]
+                ).reshape(count_x, count_y, 32, 256)
+                at = (pl.ds(xo, count_x), pl.ds(yo, count_y), pl.ds(32 * zp, 32))
+                if (dx, dy) == (1, 1):
+                    near[at] = value
+                else:
+                    near[at] += value
+
     loads[5].wait()
     for level in range(2):
         for e in range(32):
@@ -377,41 +399,50 @@
 
     lax.fori_loop(1, ny * nz, part_start, 0)
 
-    forward(1)
-    forward(2)
-
     group = lax.broadcasted_iota(jnp.int32, (48, 128), 1)
     even_z = (group % 64) < 32
     first_y = group < 64
 
-    def shifts(buf, side, x):
-        def ahead_y(a, b):
-            return jnp.where(first_y, pltpu.roll(a, 64, 1), pltpu.roll(b, 64, 1))
-
-        plain = [[buf[0, x, yp, zp] for zp in range(side)] for yp in range(side)]
-        moved = []
+    def ahead_y(a, b):
+        return jnp.where(first_y, pltpu.roll(a, 64, 1), pltpu.roll(b, 64, 1))
+
+    def shifts(buf, side, x, inner):
+        middle_rows = range(1, side - 1)
         for yp in range(side):
-            down_z = [pltpu.roll(v, 96, 1) for v in plain[yp][:-1]]
-            up_z = [pltpu.roll(v, 32, 1) for v in plain[yp][1:]]
-            moved.append([jnp.where(even_z, a, b) for a, b in zip(down_z, up_z)])
-            for zp in range(side - 1):
-                buf[1, x, yp, zp] = moved[yp][zp]
-        for kind, rows in ((2, plain), (3, moved)):
-            turned = [[pltpu.roll(v, 64, 1) for v in row] for row in rows]
-            for yp in range(side - 1):
-                for zp in range(len(rows[0])):
-                    buf[kind, x, yp, zp] = jnp.where(
-                        first_y, turned[yp][zp], turned[yp + 1][zp]
-                    )
-
+            if (yp in middle_rows) == inner:
+                line = [buf[0, x, yp, zp] for zp in range(side)]
+                down_z = [pltpu.roll(v, 96, 1) for v in line[:-1]]
+                up_z = [pltpu.roll(v, 32, 1) for v in line[1:]]
+                for zp in range(side - 1):
+                    buf[1, x, yp, zp] = jnp.where(even_z, down_z[zp], up_z[zp])
+        for yp in range(side - 1):
+            if (yp in middle_rows and yp + 1 in middle_rows) == inner:
+                for zp in range(side):
+                    buf[2, x, yp, zp] = ahead_y(buf[0, x, yp, zp], buf[0, x, yp + 1, zp])
+                for zp in range(side - 1):
+                    buf[3, x, yp, zp] = ahead_y(buf[1, x, yp, zp], buf[1, x, yp + 1, zp])
+
+    def shift_all(buf, planes_x, side, inner):
+        def step(x, carry):
+            shifts(buf, side, x, inner)
+            return carry
+
+        lax.fori_loop(0, planes_x, step, 0, unroll=planes_x // 2)
+
+    forward(1)
+    forward_outer(1)
+    forward(2)
+    forward_outer(2)
+    middle(1)
+    shift_all(mom, 8, 4, True)
+    middle(2)
+    shift_all(one, 6, 3, True)
     hand_over(1)
+    forward(0)
     finish(1)
-
-    def shift_mom(x, carry):
-        shifts(mom, 4, x)
-        return carry
-
-    lax.fori_loop(0, 8, shift_mom, 0)
+    shift_all(mom, 8, 4, False)
+    forward_outer(0)
+    hand_over(2)
     flat_mom = mom.reshape(4 * 8 * 4 * 4, 48, 128)
 
     def leaf_list(t, carry):
@@ -426,18 +457,13 @@
             down[x, 2 * yp + zp] = local[:, 128 * zp : 128 * zp + 128]
         return carry
 
-    lax.fori_loop(0, 4, leaf_list, 0)
-    hand_over(2)
-    forward(0)
-    lax.fori_loop(4, 8, leaf_list, 0)
+    lax.fori_loop(0, 4, leaf_list, 0, unroll=4)
+    hand_over(0)
+    lax.fori_loop(4, 8, leaf_list, 0, unroll=4)
 
     finish(2)
 
-    def shift_one(x, carry):
-        shifts(one, 3, x)
-        return carry
-
-    lax.fori_loop(0, 6, shift_one, 0)
+    shift_all(one, 6, 3, False)
     flat_one = one.reshape(4 * 6 * 3 * 3, 48, 128)
     windows = [
         jnp.concatenate([flat_one[base[32 + e] + cx * 9] for e in range(32)], axis=0)
@@ -475,33 +501,28 @@
                         row = 64 * y2 + 32 * z2
                         near[
                             x, 2 * yp + y2, 32 * zp : 32 * zp + 32, 128 * z2 : 128 * z2 + 128
-                        ] = far[row : row + 32]
-        return carry
-
-    lax.fori_loop(0, 4, far_x, 0)
-
-    for name in ("own", "low", "high"):
-        sides[0][name].wait_recv()
-
-    def lhs(x, ys, count):
-        parts = []
-        for step in range(3):
-            rows = [
-                jnp.concatenate([ext[x + step, pl.ds(ys, count), 2 * zp + j] for j in range(4)], axis=2)
-                for zp in range(2)
-            ]
-            stacked = jnp.stack(rows, axis=1)
-            parts.append(stacked.reshape(count * 64, 512))
-        return parts
-
-    def near_x(x, carry):
-        for dy, ys, count, row in ((1, 1, 4, 0), (0, 1, 3, 1), (2, 2, 3, 0)):
-            acc = sum(dot(v, toep[3 * step + dy]) for step, v in enumerate(lhs(x, ys, count)))
-            near[x, row : row + count] += acc.reshape(count, 64, 256)
-        return carry
-
-    lax.fori_loop(0, 4, near_x, 0)
-    hand_over(0)
+                        ] += far[row : row + 32]
+        return carry
+
+    lax.fori_loop(0, 4, far_x, 0, unroll=4)
+
+    middle(0)
+    for dy, (yo, count_y, yi) in INNER.items():
+        ys, rows_y = pl.ds(yi, count_y), pl.ds(yo, count_y)
+        for zp, z, column in ((0, 0, 0), (1, 5, 128)):
+            source_z = jnp.concatenate(
+                [boxes(pl.ds(dx, 4), ys, (z,)) for dx in range(3)], axis=1
+            )
+            taps = jnp.concatenate(
+                [toep[3 * dx + dy, 384 * zp : 384 * zp + 128, column : column + 128] for dx in range(3)],
+                axis=0,
+            )
+            value = dot(source_z, taps).reshape(4, count_y, 32, 128)
+            near[:, rows_y, pl.ds(32 * zp, 32), pl.ds(column, 128)] += value
+        for dx, xe, xo in ((0, 0, 0), (2, 5, 3)):
+            for zp, zs, rows in ((0, (1, 2, 3), pl.ds(128, 384)), (1, (2, 3, 4), pl.ds(0, 384))):
+                value = dot(boxes(pl.ds(xe, 1), ys, zs), toep[3 * dx + dy, rows])
+                near[xo, rows_y, pl.ds(32 * zp, 32)] += value.reshape(count_y, 32, 256)
 
     def write(y):
         for x in range(4):

time: 47.2 us -> 43.3 us (0.917)
  the two profiles are of different devices: /device:TPU:2 before, /device:TPU:1 now
where the time goes in v3:
time: 43.3 us; the launch traced here: 43.1 us
  Pallas kernels  40.8 us (94%)
  local copies, waits for them, and re-layouts  2.29 us (5%)
    pallas_call x1, Pallas kernels, body(): pl.pallas_call(functools.partial(kernel, sizes), out_shape=jax.ShapeDtype...  40.8 us
    unnamed x1, local copies, waits for them, and re-layouts  2.29 us

profile of v3, /device:TPU:1, one launch (start us, length us, event | category | flops | bytes accessed | tf_op | source)
XLA Modules:
  0.0 43.1 jit_solution(5616742840761667722)
XLA Ops:
  0.0 40.8 %shard_map.91 = f32[4,4,4,32,128]{4,3,2,1,0:T(8,128)} custom-call(s32[4,4,4]{2,1,0:T(4,128)} %counts.1, s32[3,27]{1,0:T(4,128)} %bitcast.3, s32[3,2,32]{2,1,0:T(2,128)} %bitcast.2, bf16[4,4,4,32,128]{4,3,2,1,0:T(8,128)(2,1)} %charges.1, bf16[27,128,128]{2,1,0:T(8,128)(2,1)} %near_blocks.1, bf16[48,128]{1,0:T(8,128)(2,1)} %basis_hbm.1, ...), custom_call_target="tpu_custom_call" | custom-call | tf_op jit(solution)/shard_map/pallas_call | solution.py:587
  40.8 2.3 %copy.11 = f32[4,4,4,32,128]{4,3,2,1,0:T(8,128)} copy(f32[4,4,4,32,128]{4,3,2,1,0:T(8,128)} %shard_map.91) | data formatting | bytes 2097152

commit v4 on v3

--- a/solution.py
+++ b/solution.py
@@ -297,7 +297,6 @@
     start_slab(1)
     start_plane(2)
     start_slab(2)
-    start_plane(0)
     start_slab(0)
 
     codes = [9 * near_off[0, s] + 3 * near_off[1, s] + near_off[2, s] + 13 for s in range(27)]
@@ -324,6 +323,42 @@
             else:
                 base[32 + e] = ((kind * 6 + ox) * 3 + half_y) * 3 + half_z
 
+    loads[4].wait()
+
+    def gather_wait(d, carry):
+        gather_copy(d).wait_recv()
+        return carry
+
+    lax.fori_loop(1, nx, gather_wait, 0)
+
+    def partial(dy, carry):
+        acc = jnp.zeros((192, 32), F32)
+        for d in range(nx):
+            mats = coarse[(nx - d) % nx, dy].reshape(192, 48)
+            acc = acc + dot(mats, unpack(gathered[d]))
+        for dz in range(4):
+            part_out[4 * dy + dz] = pack(acc[48 * dz : 48 * dz + 48]).astype(BF)
+        return carry
+
+    lax.fori_loop(0, 4, partial, 0)
+
+    def part_copy(d):
+        return pltpu.make_async_remote_copy(
+            src_ref=part_out.at[d],
+            dst_ref=part_in.at[d],
+            send_sem=p_send.at[d],
+            recv_sem=p_recv.at[d],
+            device_id=device(0, -(d // nz), -(d % nz)),
+            device_id_type=MESH,
+        )
+
+    def part_start(d, carry):
+        part_copy(d).start()
+        return carry
+
+    lax.fori_loop(1, ny * nz, part_start, 0)
+    start_plane(0)
+
     loads[3].wait()
 
     def build(c, carry):
@@ -340,6 +375,11 @@
         return carry
 
     lax.fori_loop(0, 9, build, 0)
+
+    loads[5].wait()
+    for level in range(2):
+        for e in range(32):
+            packed[level, :, 48 * e : 48 * e + 48] = coupling[level, e]
 
     def boxes(xs, ys, zs):
         parts = [ext[xs, ys, z] for z in zs]
@@ -359,45 +399,6 @@
                 else:
                     near[at] += value
 
-    loads[5].wait()
-    for level in range(2):
-        for e in range(32):
-            packed[level, :, 48 * e : 48 * e + 48] = coupling[level, e]
-
-    loads[4].wait()
-
-    def gather_wait(d, carry):
-        gather_copy(d).wait_recv()
-        return carry
-
-    lax.fori_loop(1, nx, gather_wait, 0)
-
-    def partial(dy, carry):
-        acc = jnp.zeros((192, 32), F32)
-        for d in range(nx):
-            mats = coarse[(nx - d) % nx, dy].reshape(192, 48)
-            acc = acc + dot(mats, unpack(gathered[d]))
-        for dz in range(4):
-            part_out[4 * dy + dz] = pack(acc[48 * dz : 48 * dz + 48])
-        return carry
-
-    lax.fori_loop(0, 4, partial, 0)
-
-    def part_copy(d):
-        return pltpu.make_async_remote_copy(
-            src_ref=part_out.at[d],
-            dst_ref=part_in.at[d],
-            send_sem=p_send.at[d],
-            recv_sem=p_recv.at[d],
-            device_id=device(0, -(d // nz), -(d % nz)),
-            device_id_type=MESH,
-        )
-
-    def part_start(d, carry):
-        part_copy(d).start()
-        return carry
-
-    lax.fori_loop(1, ny * nz, part_start, 0)
 
     group = lax.broadcasted_iota(jnp.int32, (48, 128), 1)
     even_z = (group % 64) < 32
@@ -439,6 +440,14 @@
     shift_all(one, 6, 3, True)
     hand_over(1)
     forward(0)
+
+    for dy, (yo, count_y, yi) in INNER.items():
+        ys, rows_y = pl.ds(yi, count_y), pl.ds(yo, count_y)
+        for dx, xe, xo in ((0, 0, 0), (2, 5, 3)):
+            for zp, zs, rows in ((0, (1, 2, 3), pl.ds(128, 384)), (1, (2, 3, 4), pl.ds(0, 384))):
+                value = dot(boxes(pl.ds(xe, 1), ys, zs), toep[3 * dx + dy, rows])
+                near[xo, rows_y, pl.ds(32 * zp, 32)] += value.reshape(count_y, 32, 256)
+
     finish(1)
     shift_all(mom, 8, 4, False)
     forward_outer(0)
@@ -476,9 +485,9 @@
         return carry
 
     lax.fori_loop(1, ny * nz, part_wait, 0)
-    total = part_out[0]
+    total = part_out[0].astype(F32)
     for d in range(1, ny * nz):
-        total = total + part_in[d]
+        total = total + part_in[d].astype(F32)
     local_two = unpack(total).astype(BF)
     for cx in range(2):
         spread = jnp.concatenate(
@@ -519,10 +528,6 @@
             )
             value = dot(source_z, taps).reshape(4, count_y, 32, 128)
             near[:, rows_y, pl.ds(32 * zp, 32), pl.ds(column, 128)] += value
-        for dx, xe, xo in ((0, 0, 0), (2, 5, 3)):
-            for zp, zs, rows in ((0, (1, 2, 3), pl.ds(128, 384)), (1, (2, 3, 4), pl.ds(0, 384))):
-                value = dot(boxes(pl.ds(xe, 1), ys, zs), toep[3 * dx + dy, rows])
-                near[xo, rows_y, pl.ds(32 * zp, 32)] += value.reshape(count_y, 32, 256)
 
     def write(y):
         for x in range(4):
@@ -604,8 +609,8 @@
             pltpu.VMEM((4, 4, 64, 256), F32),
             pltpu.VMEM((4, 4, 4, 32, 128), F32),
             pltpu.VMEM((nx, 16, 128), BF),
-            pltpu.VMEM((ny * nz, 16, 128), F32),
-            pltpu.VMEM((ny * nz, 16, 128), F32),
+            pltpu.VMEM((ny * nz, 16, 128), BF),
+            pltpu.VMEM((ny * nz, 16, 128), BF),
             pltpu.VMEM((4, 4, 48, 128), F32),
             pltpu.SMEM((64,), jnp.int32),
             pltpu.SMEM((64,), jnp.int32),

time: 43.3 us -> 41.5 us (0.958)
  the two profiles are of different devices: /device:TPU:1 before, /device:TPU:2 now
where the time goes in v4:
time: 41.5 us; the launch traced here: 41.3 us
  Pallas kernels  39 us (94%)
  local copies, waits for them, and re-layouts  2.29 us (6%)
    pallas_call x1, Pallas kernels, body(): pl.pallas_call(functools.partial(kernel, sizes), out_shape=jax.ShapeDtype...  39 us
    unnamed x1, local copies, waits for them, and re-layouts  2.29 us

profile of v4, /device:TPU:2, one launch (start us, length us, event | category | flops | bytes accessed | tf_op | source)
XLA Modules:
  0.0 41.3 jit_solution(13509924237718539492)
XLA Ops:
  0.0 39.0 %shard_map.91 = f32[4,4,4,32,128]{4,3,2,1,0:T(8,128)} custom-call(s32[4,4,4]{2,1,0:T(4,128)} %counts.1, s32[3,27]{1,0:T(4,128)} %bitcast.3, s32[3,2,32]{2,1,0:T(2,128)} %bitcast.2, bf16[4,4,4,32,128]{4,3,2,1,0:T(8,128)(2,1)} %charges.1, bf16[27,128,128]{2,1,0:T(8,128)(2,1)} %near_blocks.1, bf16[48,128]{1,0:T(8,128)(2,1)} %basis_hbm.1, ...), custom_call_target="tpu_custom_call" | custom-call | tf_op jit(solution)/shard_map/pallas_call | solution.py:592
  39.0 2.3 %copy.11 = f32[4,4,4,32,128]{4,3,2,1,0:T(8,128)} copy(f32[4,4,4,32,128]{4,3,2,1,0:T(8,128)} %shard_map.91) | data formatting | bytes 2097152

commit v5 on v4

--- a/solution.py
+++ b/solution.py
@@ -114,7 +114,7 @@
             )
         )
     ]
-    for copy in loads:
+    for copy in loads[:3]:
         copy.start()
 
     barrier = pltpu.get_barrier_semaphore()
@@ -160,10 +160,13 @@
         plane = {}
         for dx in (-1, 0, 1):
             rx = (source(ax, dx), target(ax, dx)) if dx else (own(ax), own(ax))
+            far = rx
+            if f == 2 and dx:
+                far = (pl.ds(2, 1), pl.ds(0, 1)) if dx > 0 else (pl.ds(3, 1), pl.ds(5, 1))
             if dx:
                 plane[dx, 0] = remote(
                     f, (dx + 1) // 2, device(dx, 0, 0),
-                    (rx[0], own(ay), own(az)), (rx[1], own(ay), own(az)),
+                    (far[0], own(ay), own(az)), (far[1], own(ay), own(az)),
                 )
             plane[dx, 1] = remote(
                 f, 3 + dx, device(dx, 0, flip),
@@ -237,6 +240,8 @@
             sides[f][dy].wait_recv()
 
     loads[0].wait()
+    for copy in loads[3:]:
+        copy.start()
     lane = lax.broadcasted_iota(jnp.int32, (32, 128), 1)
 
     def mask_x(x, carry):
@@ -261,14 +266,17 @@
 
     lax.fori_loop(0, 4, leaf_x, 0)
 
-    for cx in range(2):
+    def merge(x):
         acc = jnp.zeros((48, 128), F32)
         for i in range(2):
-            quads = [mom[0, 2 * cx + i + 2, cy + 1, cz + 1] for cy in range(2) for cz in range(2)]
+            quads = [mom[0, 2 * x - 2 + i, cy + 1, cz + 1] for cy in range(2) for cz in range(2)]
             for jl in range(4):
                 kids = jnp.concatenate([q[:, 32 * jl : 32 * jl + 32] for q in quads], axis=1)
                 acc = acc + dot(transfer[4 * i + jl], kids)
-        one[0, cx + 2, 1, 1] = acc.astype(BF)
+        one[0, x, 1, 1] = acc.astype(BF)
+
+    for x in (2, 3):
+        merge(x)
 
     acc = jnp.zeros((48, 32), F32)
     for i in range(2):
@@ -432,6 +440,8 @@
 
     forward(1)
     forward_outer(1)
+    for x in (1, 4):
+        merge(x)
     forward(2)
     forward_outer(2)
     middle(1)

time: 41.5 us -> 41.4 us (level)
  no operation moved by 1% of the time
where the time goes in v5:
time: 41.4 us; the launch traced here: 41.3 us
  Pallas kernels  39 us (94%)
  local copies, waits for them, and re-layouts  2.29 us (6%)
    pallas_call x1, Pallas kernels, body(): pl.pallas_call(functools.partial(kernel, sizes), out_shape=jax.ShapeDtype...  39 us
    unnamed x1, local copies, waits for them, and re-layouts  2.29 us

profile of v5, /device:TPU:2, one launch (start us, length us, event | category | flops | bytes accessed | tf_op | source)
XLA Modules:
  0.0 41.3 jit_solution(10681078300185302099)
XLA Ops:
  0.0 39.0 %shard_map.91 = f32[4,4,4,32,128]{4,3,2,1,0:T(8,128)} custom-call(s32[4,4,4]{2,1,0:T(4,128)} %counts.1, s32[3,27]{1,0:T(4,128)} %bitcast.3, s32[3,2,32]{2,1,0:T(2,128)} %bitcast.2, bf16[4,4,4,32,128]{4,3,2,1,0:T(8,128)(2,1)} %charges.1, bf16[27,128,128]{2,1,0:T(8,128)(2,1)} %near_blocks.1, bf16[48,128]{1,0:T(8,128)(2,1)} %basis_hbm.1, ...), custom_call_target="tpu_custom_call" | custom-call | tf_op jit(solution)/shard_map/pallas_call | solution.py:602
  39.0 2.3 %copy.11 = f32[4,4,4,32,128]{4,3,2,1,0:T(8,128)} copy(f32[4,4,4,32,128]{4,3,2,1,0:T(8,128)} %shard_map.91) | data formatting | bytes 2097152
